TPU v7x, 32 devices: a whole 2x2x4 slice. The times are simulated.
32 devices in a mesh: fsdp: 16 (over z, y, core), tp: 2 (over x).
Axes of the slice: x: 2, y: 2, z: 4, core: 2. Of those that a mesh axis runs over, the one named last changes fastest.
Arguments:
- hidden: bfloat16 [32, 5120], P(None, 'fsdp'), may hold values from -20 to 20
- query_weight: bfloat16 [5120, 5120], P(None, ('tp', 'fsdp')), may hold values from -0.078125 to 0.078125
- key_weight: bfloat16 [5120, 1024], P(None, ('tp', 'fsdp')), may hold values from -0.078125 to 0.078125
- value_weight: bfloat16 [5120, 1024], P(None, ('tp', 'fsdp')), may hold values from -0.078125 to 0.078125
- output_weight: bfloat16 [5120, 5120], P(('tp', 'fsdp')), may hold values from -0.078125 to 0.078125
- gate_weight: bfloat16 [5120, 27648], P(None, ('tp', 'fsdp')), may hold values from -0.078125 to 0.078125
- up_weight: bfloat16 [5120, 27648], P(None, ('tp', 'fsdp')), may hold values from -0.078125 to 0.078125
- down_weight: bfloat16 [27648, 5120], P(('tp', 'fsdp')), may hold values from -0.0390625 to 0.0390625
- history: float32 [7, 1024], replicated, may hold values from 0.0001 to 1, as said below
- slot: int32 [1], replicated, may hold values from 0 to 1023
- lengths: int32 [32], P('fsdp'), may hold values from 512 to 4096, as said below
- key_cache: bfloat16 [32, 4096, 1024], P('fsdp', None, 'tp'), may hold values from -1000 to 1000
- value_cache: bfloat16 [32, 4096, 1024], P('fsdp', None, 'tp'), may hold values from -6 to 6
Outputs:
- attention_out: bfloat16 [32, 5120], P('fsdp', 'tp')
- query_rollout: bfloat16 [5120, 5120], P('fsdp', 'tp')
- key_rollout: bfloat16 [5120, 1024], P('fsdp', 'tp')
- value_rollout: bfloat16 [5120, 1024], P('fsdp', 'tp')
- output_rollout: bfloat16 [5120, 5120], P('tp', 'fsdp')
- gate_rollout: bfloat16 [5120, 27648], P('fsdp', 'tp')
- up_rollout: bfloat16 [5120, 27648], P('fsdp', 'tp')
- down_rollout: bfloat16 [27648, 5120], P('tp', 'fsdp')
- new_history: float32 [7, 1024], replicated
Inputs may be any that keep to these rules, and one draw needn't show every extreme that they name: `history`: strictly positive. `lengths`: some sequence has all 4096 slots valid.
All inputs are finite; a program needn't handle non-finite values.
Results may differ from a plain program's by a relative error of at most 0.012.
The roundings to bfloat16 on the way count: a program that leaves them out, or rounds other values in their place, can miss the bound.
Values may be sent and summed in bfloat16 or wider, within the bound.
No kernel may reach another device: no remote copies, remote signals or barrier semaphores. Data moves between devices by JAX's collectives and lax.ppermute only.
A program may use at most 192 MiB of HBM per device.

v0:
```python
import jax
import jax.numpy as jnp
from jax import lax
from jax.sharding import PartitionSpec as P

D = 5120
HEADS = 40
KV_HEADS = 8
HEAD_DIM = 128


target_peak = 4.0
norm_eps = 1e-06
rope_theta = 1000000.0


def largest(tensor):
    return jnp.max(jnp.abs(tensor.astype(jnp.float32)))


def scaling(peaks, history, slot):
    marked = lax.broadcasted_iota(jnp.int32, history.shape, 1) == slot[0]
    kept = jnp.max(jnp.where(marked, jnp.zeros_like(history), history), axis=1)
    return (target_peak / jnp.maximum(peaks, kept), jnp.where(marked, peaks[:, None], history))


def quantize(tensor, factor):
    return (tensor.astype(jnp.float32) * factor).astype(jnp.bfloat16)


def rotate(vectors, positions):
    half_dim = vectors.shape[-1] // 2
    ladder = jnp.arange(half_dim, dtype=jnp.float32)
    spread = rope_theta ** (-2.0 * ladder / vectors.shape[-1])
    angle = positions.astype(jnp.float32)[:, None] * spread[None, :]
    cosine = jnp.cos(angle)[:, None, :]
    sine = jnp.sin(angle)[:, None, :]
    first = vectors[..., :half_dim]
    second = vectors[..., half_dim:]
    return jnp.concatenate(
        [first * cosine - second * sine, second * cosine + first * sine], axis=-1
    )


def regroup(query_part, key_part, value_part, output_part, gate_part, up_part, down_part):
    columns = (
        lax.all_to_all(query_part, "fsdp", split_axis=0, concat_axis=1, tiled=True),
        lax.all_to_all(key_part, "fsdp", split_axis=0, concat_axis=1, tiled=True),
        lax.all_to_all(value_part, "fsdp", split_axis=0, concat_axis=1, tiled=True),
        lax.all_to_all(gate_part, "fsdp", split_axis=0, concat_axis=1, tiled=True),
        lax.all_to_all(up_part, "fsdp", split_axis=0, concat_axis=1, tiled=True),
    )
    rowwise = (
        lax.all_to_all(output_part, "fsdp", split_axis=1, concat_axis=0, tiled=True),
        lax.all_to_all(down_part, "fsdp", split_axis=1, concat_axis=0, tiled=True),
    )
    return (columns[0], columns[1], columns[2], rowwise[0], columns[3], columns[4], rowwise[1])


def attend(query, key_new, value_new, key_cache, value_cache, lengths):
    count_seq = query.shape[0]
    kv_count = query.shape[1]
    head_dim = query.shape[3]
    cache_len = key_cache.shape[1]
    keys = key_cache.reshape(count_seq, cache_len, kv_count, head_dim)
    values = value_cache.reshape(count_seq, cache_len, kv_count, head_dim)
    scale = head_dim ** (-0.5)
    scores = jnp.einsum("bkgd,bjkd->bkgj", query, keys, preferred_element_type=jnp.float32) * scale
    own = (
        jnp.sum(query.astype(jnp.float32) * key_new.astype(jnp.float32)[:, :, None, :], axis=-1)
        * scale
    )
    valid = (lax.broadcasted_iota(jnp.int32, (count_seq, cache_len), 1) < lengths[:, None])[
        :, None, None, :
    ]
    top = jnp.maximum(jnp.max(jnp.where(valid, scores, -1e30), axis=-1), own)
    weights = jnp.where(valid, jnp.exp(scores - top[..., None]), 0.0)
    own_weight = jnp.exp(own - top)
    total = jnp.sum(weights, axis=-1) + own_weight
    probs = (weights / total[..., None]).astype(jnp.bfloat16)
    own_prob = (own_weight / total).astype(jnp.bfloat16)
    mixed = jnp.einsum("bkgj,bjkd->bkgd", probs, values, preferred_element_type=jnp.float32)
    mixed = (
        mixed
        + own_prob.astype(jnp.float32)[..., None] * value_new.astype(jnp.float32)[:, :, None, :]
    )
    return mixed.astype(jnp.bfloat16).reshape(count_seq, -1)


def per_device(
    hidden,
    query_weight,
    key_weight,
    value_weight,
    output_weight,
    gate_weight,
    up_weight,
    down_weight,
    history,
    slot,
    lengths,
    key_cache,
    value_cache,
):
    trainer = (
        query_weight,
        key_weight,
        value_weight,
        output_weight,
        gate_weight,
        up_weight,
        down_weight,
    )
    peaks = jnp.stack([lax.pmax(largest(tensor), ("fsdp", "tp")) for tensor in trainer])
    factors, new_history = scaling(peaks, history, slot)
    arrived = regroup(
        query_weight, key_weight, value_weight, output_weight, gate_weight, up_weight, down_weight
    )
    rollout = tuple((quantize(arrived[number], factors[number]) for number in range(7)))
    (
        query_rollout,
        key_rollout,
        value_rollout,
        output_rollout,
        gate_rollout,
        up_rollout,
        down_rollout,
    ) = rollout
    widened = hidden.astype(jnp.float32)
    squares = jnp.sum(widened * widened, axis=1)
    joined = jnp.concatenate([query_rollout, key_rollout, value_rollout], axis=1)
    partial_value = jnp.dot(hidden, joined, preferred_element_type=jnp.float32)
    summed, total_sq = (
        lax.psum_scatter(partial_value, "fsdp", scatter_dimension=0, tiled=True),
        lax.psum_scatter(squares, "fsdp", scatter_dimension=0, tiled=True),
    )
    inv_rms = lax.rsqrt(total_sq / D + norm_eps)[:, None]
    width_q = query_rollout.shape[1]
    width_k = key_rollout.shape[1]
    query = summed[:, :width_q] * inv_rms / factors[0]
    key_new = summed[:, width_q : width_q + width_k] * inv_rms / factors[1]
    value_new = summed[:, width_q + width_k :] * inv_rms / factors[2]
    count_seq = summed.shape[0]
    query = rotate(query.reshape(count_seq, -1, HEAD_DIM), lengths).astype(jnp.bfloat16)
    query = query.reshape(count_seq, -1, HEADS // KV_HEADS, HEAD_DIM)
    key_new = rotate(key_new.reshape(count_seq, -1, HEAD_DIM), lengths).astype(jnp.bfloat16)
    value_new = value_new.reshape(count_seq, -1, HEAD_DIM).astype(jnp.bfloat16)
    attention_out = attend(query, key_new, value_new, key_cache, value_cache, lengths)
    return (
        attention_out,
        query_rollout,
        key_rollout,
        value_rollout,
        output_rollout,
        gate_rollout,
        up_rollout,
        down_rollout,
        new_history,
    )


def solution(mesh):
    return jax.shard_map(
        per_device,
        mesh=mesh,
        in_specs=(
            P(None, "fsdp"),
            P(None, ("tp", "fsdp")),
            P(None, ("tp", "fsdp")),
            P(None, ("tp", "fsdp")),
            P(("tp", "fsdp"), None),
            P(None, ("tp", "fsdp")),
            P(None, ("tp", "fsdp")),
            P(("tp", "fsdp"), None),
            P(),
            P(),
            P("fsdp"),
            P("fsdp", None, "tp"),
            P("fsdp", None, "tp"),
        ),
        out_specs=(
            P("fsdp", "tp"),
            P("fsdp", "tp"),
            P("fsdp", "tp"),
            P("fsdp", "tp"),
            P("tp", "fsdp"),
            P("fsdp", "tp"),
            P("fsdp", "tp"),
            P("tp", "fsdp"),
            P(),
        ),
        check_vma=False,
    )
```

profile of v0, /device:TPU:0, one launch (start us, length us, event | category | flops | bytes accessed | tf_op | source)
XLA Modules:
  0.0 1055.8 jit_solution(7451371705270785353)
XLA Ops:
  9.3 7.4 all-to-all-start.1
  18.9 10.0 all-to-all-done.1
  38.2 7.1 all-to-all-done.2
  45.3 4.4 all-to-all-start
  54.8 33.7 %all-to-all-done = bf16[16,320,160]{1,2,0:T(8,128)(2,1)} async-done(((bf16[16,320,160]{1,2,0:T(8,128)(2,1)}), bf16[16,320,160]{1,2,0:T(8,128)(2,1)}, u32[]{:S(2)}, u32[]{:S(2)}) %all-to-all-start) | async-done | bytes 1638432 | tf_op jit(solution)/shard_map/all_to_all | solution.py:47
  88.4 10.7 %all-to-all-start.3 = ((bf16[160,16,320]{2,0,1:T(8,128)(2,1)}), bf16[160,16,320]{2,0,1:T(8,128)(2,1)S(1)}, u32[]{:S(2)}, u32[]{:S(2)}) async-start(bf16[160,16,320]{2,0,1:T(8,128)(2,1)} %copy.77), calls=%async_computation.3 | async-start | bytes 3932160 | tf_op jit(solution)/shard_map/all_to_all | solution.py:54
  99.1 12.7 %copy.78 = bf16[5120,864]{1,0:T(8,128)(2,1)} copy(bf16[5120,864]{0,1:T(8,128)(2,1)} %param.18) | data formatting | bytes 17694720 | tf_op args[5]
  111.8 26.0 %all-to-all-done.3 = bf16[160,16,320]{2,0,1:T(8,128)(2,1)S(1)} async-done(((bf16[160,16,320]{2,0,1:T(8,128)(2,1)}), bf16[160,16,320]{2,0,1:T(8,128)(2,1)S(1)}, u32[]{:S(2)}, u32[]{:S(2)}) %all-to-all-start.3) | async-done | bytes 1638432 | tf_op jit(solution)/shard_map/all_to_all | solution.py:54
  139.1 10.7 %all-to-all-start.4 = ((bf16[16,320,864]{2,1,0:T(8,128)(2,1)}), bf16[16,320,864]{2,1,0:T(8,128)(2,1)}, u32[]{:S(2)}, u32[]{:S(2)}) async-start(bf16[16,320,864]{2,1,0:T(8,128)(2,1)} %bitcast.74), calls=%async_computation.4 | async-start | bytes 18350080 | tf_op jit(solution)/shard_map/all_to_all | solution.py:50
  149.8 12.7 %copy.80 = bf16[5120,864]{1,0:T(8,128)(2,1)} copy(bf16[5120,864]{0,1:T(8,128)(2,1)} %param.19) | data formatting | bytes 17694720 | tf_op args[6]
  162.5 151.6 %all-to-all-done.4 = bf16[16,320,864]{2,1,0:T(8,128)(2,1)} async-done(((bf16[16,320,864]{2,1,0:T(8,128)(2,1)}), bf16[16,320,864]{2,1,0:T(8,128)(2,1)}, u32[]{:S(2)}, u32[]{:S(2)}) %all-to-all-start.4) | async-done | bytes 8847392 | tf_op jit(solution)/shard_map/all_to_all | solution.py:50
  314.1 39.7 %all-to-all-start.5 = ((bf16[16,320,864]{2,1,0:T(8,128)(2,1)}), bf16[16,320,864]{2,1,0:T(8,128)(2,1)}, u32[]{:S(2)}, u32[]{:S(2)}) async-start(bf16[16,320,864]{2,1,0:T(8,128)(2,1)} %bitcast.75), calls=%async_computation.5 | async-start | bytes 18350080 | tf_op jit(solution)/shard_map/all_to_all | solution.py:51
  353.8 12.7 %copy.82 = bf16[864,5120]{0,1:T(8,128)(2,1)} copy(bf16[864,5120]{1,0:T(8,128)(2,1)} %param.20) | data formatting | bytes 17694720 | tf_op args[7]
  366.5 151.6 %all-to-all-done.5 = bf16[16,320,864]{2,1,0:T(8,128)(2,1)} async-done(((bf16[16,320,864]{2,1,0:T(8,128)(2,1)}), bf16[16,320,864]{2,1,0:T(8,128)(2,1)}, u32[]{:S(2)}, u32[]{:S(2)}) %all-to-all-start.5) | async-done | bytes 8847392 | tf_op jit(solution)/shard_map/all_to_all | solution.py:51
  518.1 40.0 %all-to-all-start.6 = ((bf16[864,16,320]{0,2,1:T(8,128)(2,1)}), bf16[864,16,320]{0,2,1:T(8,128)(2,1)}, u32[]{:S(2)}, u32[]{:S(2)}) async-start(bf16[864,16,320]{0,2,1:T(8,128)(2,1)} %bitcast.73), calls=%async_computation.6 | async-start | bytes 18350080 | tf_op jit(solution)/shard_map/all_to_all | solution.py:55
  563.5 5.9 abs_reduce_fusion.2
  569.5 5.8 abs_reduce_fusion.1
  577.7 201.4 %all-reduce.2 = (f32[1]{0:T(128)}, f32[1]{0:T(128)}, f32[1]{0:T(128)}, f32[1]{0:T(128)}, f32[1]{0:T(128)}, /*index=5*/f32[1]{0:T(128)}, f32[1]{0:T(128)}) all-reduce(f32[1]{0:T(128)} %bitcast, f32[1]{0:T(128)} %bitcast.1, f32[1]{0:T(128)} %bitcast.2, f32[1]{0:T(128)} %bitcast.3, ...), channel_id=1, replica_groups=mesh['fsdp'=16,'tp'=2] {'fsdp','tp'}, use_global_device_ids=true, to_apply=%region_1.0 | all-reduce | flops 7 | bytes 56 | tf_op jit(solution)/shard_map/pmax | solution.py:114
  781.0 4.5 stack.31
  785.7 31.4 %all-reduce.1 = f32[32]{0:T(128)S(1)} all-reduce(f32[32]{0:T(128)S(1)} %multiply_reduce_fusion), channel_id=3, replica_groups=mesh['fsdp'=16,'tp'=2] {'fsdp'}, use_global_device_ids=true, to_apply=%region_17.18.clone | all-reduce | flops 32 | bytes 256
  835.6 81.8 %all-reduce.5.cloned.1.call-done = f32[32,3584]{1,0:T(8,128)} async-done(((f32[32,3584]{1,0:T(8,128)}), f32[32,3584]{1,0:T(8,128)}) %all-reduce.5.cloned.1.call-update) | async-done | bytes 458768
  921.6 5.8 select_reduce_fusion
  927.9 4.7 fusion.20
  933.2 9.7 fusion
  943.0 12.4 %copy.79 = bf16[320,16,864]{2,1,0:T(8,128)(2,1)} copy(bf16[320,16,864]{2,0,1:T(8,128)(2,1)} %fusion) | data formatting | bytes 17694720 | tf_op jit(solution)/shard_map/convert_element_type | solution.py:28
  955.4 16.3 %convert_element_type.218 = bf16[320,13824]{1,0:T(8,128)(2,1)} reshape(bf16[320,16,864]{2,1,0:T(8,128)(2,1)} %copy.79) | data formatting | bytes 17694720 | tf_op jit(solution)/shard_map/convert_element_type | solution.py:28
  971.7 9.8 fusion.1
  981.5 12.4 %copy.81 = bf16[320,16,864]{2,1,0:T(8,128)(2,1)} copy(bf16[320,16,864]{2,0,1:T(8,128)(2,1)} %fusion.1) | data formatting | bytes 17694720 | tf_op jit(solution)/shard_map/convert_element_type | solution.py:28
  993.9 16.4 %convert_element_type.222 = bf16[320,13824]{1,0:T(8,128)(2,1)} reshape(bf16[320,16,864]{2,1,0:T(8,128)(2,1)} %copy.81) | data formatting | bytes 17694720 | tf_op jit(solution)/shard_map/convert_element_type | solution.py:28
  1010.3 9.8 fusion.2
  1020.1 12.4 %copy.83 = bf16[16,864,320]{1,0,2:T(8,128)(2,1)} copy(bf16[16,864,320]{1,2,0:T(8,128)(2,1)} %fusion.2) | data formatting | bytes 17694720 | tf_op jit(solution)/shard_map/convert_element_type | solution.py:28
  1032.5 16.1 %convert_element_type.226 = bf16[13824,320]{0,1:T(8,128)(2,1)} reshape(bf16[16,864,320]{1,0,2:T(8,128)(2,1)} %copy.83) | data formatting | bytes 17694720 | tf_op jit(solution)/shard_map/convert_element_type | solution.py:28
  (83 shorter events, 52.1 us)
Async XLA Ops:
  9.3 19.6 %all-to-all-start.1 = ((bf16[16,320,32]{1,2,0:T(8,128)(2,1)}), bf16[16,320,32]{1,2,0:T(8,128)(2,1)S(1)}, u32[]{:S(2)}, u32[]{:S(2)}) async-start(bf16[16,320,32]{1,2,0:T(8,128)(2,1)} %copy.69), calls=%async_computation.1 | async-start | bytes 786432 | tf_op jit(solution)/shard_map/all_to_all | solution.py:48
  28.9 0.7 copy-start.3
  29.6 15.7 %all-to-all-start.2 = ((bf16[16,320,32]{1,2,0:T(8,128)(2,1)}), bf16[16,320,32]{1,2,0:T(8,128)(2,1)S(1)}, u32[]{:S(2)}, u32[]{:S(2)}) async-start(bf16[16,320,32]{1,2,0:T(8,128)(2,1)} %copy.70), calls=%async_computation.2 | async-start | bytes 786432 | tf_op jit(solution)/shard_map/all_to_all | solution.py:49
  45.3 66.5 %copy-start.5 = (bf16[16,320,32]{1,2,0:T(8,128)(2,1)}, bf16[16,320,32]{1,2,0:T(8,128)(2,1)S(1)}, u32[]{:S(2)}) copy-start(bf16[16,320,32]{1,2,0:T(8,128)(2,1)S(1)} %all-to-all-done.2) | copy-start | bytes 983044
  45.3 43.1 %all-to-all-start = ((bf16[16,320,160]{1,2,0:T(8,128)(2,1)}), bf16[16,320,160]{1,2,0:T(8,128)(2,1)}, u32[]{:S(2)}, u32[]{:S(2)}) async-start(bf16[16,320,160]{1,2,0:T(8,128)(2,1)} %copy.68), calls=%async_computation | async-start | bytes 3932160 | tf_op jit(solution)/shard_map/all_to_all | solution.py:47
  88.4 49.4 %all-to-all-start.3 = ((bf16[160,16,320]{2,0,1:T(8,128)(2,1)}), bf16[160,16,320]{2,0,1:T(8,128)(2,1)S(1)}, u32[]{:S(2)}, u32[]{:S(2)}) async-start(bf16[160,16,320]{2,0,1:T(8,128)(2,1)} %copy.77), calls=%async_computation.3 | async-start | bytes 3932160 | tf_op jit(solution)/shard_map/all_to_all | solution.py:54
  137.8 1.3 copy-start
  139.1 175.0 %all-to-all-start.4 = ((bf16[16,320,864]{2,1,0:T(8,128)(2,1)}), bf16[16,320,864]{2,1,0:T(8,128)(2,1)}, u32[]{:S(2)}, u32[]{:S(2)}) async-start(bf16[16,320,864]{2,1,0:T(8,128)(2,1)} %bitcast.74), calls=%async_computation.4 | async-start | bytes 18350080 | tf_op jit(solution)/shard_map/all_to_all | solution.py:50
  314.1 204.0 %all-to-all-start.5 = ((bf16[16,320,864]{2,1,0:T(8,128)(2,1)}), bf16[16,320,864]{2,1,0:T(8,128)(2,1)}, u32[]{:S(2)}, u32[]{:S(2)}) async-start(bf16[16,320,864]{2,1,0:T(8,128)(2,1)} %bitcast.75), calls=%async_computation.5 | async-start | bytes 18350080 | tf_op jit(solution)/shard_map/all_to_all | solution.py:51
  518.1 43.8 %copy-start.1 = (bf16[5120,160]{0,1:T(8,128)(2,1)S(1)}, bf16[5120,160]{0,1:T(8,128)(2,1)}, u32[]{:S(2)}) copy-start(bf16[5120,160]{0,1:T(8,128)(2,1)} %param.14) | copy-start | bytes 4915204
  518.1 44.6 %copy-start.2 = (bf16[160,5120]{1,0:T(8,128)(2,1)S(1)}, bf16[160,5120]{1,0:T(8,128)(2,1)}, u32[]{:S(2)}) copy-start(bf16[160,5120]{1,0:T(8,128)(2,1)} %param.17) | copy-start | bytes 4915204
  518.1 492.2 %all-to-all-start.6 = ((bf16[864,16,320]{0,2,1:T(8,128)(2,1)}), bf16[864,16,320]{0,2,1:T(8,128)(2,1)}, u32[]{:S(2)}, u32[]{:S(2)}) async-start(bf16[864,16,320]{0,2,1:T(8,128)(2,1)} %bitcast.73), calls=%async_computation.6 | async-start | bytes 18350080 | tf_op jit(solution)/shard_map/all_to_all | solution.py:55
  558.1 359.3 %all-reduce.5.cloned.1.call-start = ((), (), s32[]{:S(2)}) async-start(), calls=%async_computation.7 | async-start | bytes 917504
  563.5 11.8 %slice-start = ((s8[8847360]{0:T(1024)(128)(4,1)}), s8[4194304]{0:T(1024)(128)(4,1)S(1)}, s32[]{:S(2)}) async-start(s8[8847360]{0:T(1024)(128)(4,1)} %bitcast.76), calls=%async_computation.8 | async-start | bytes 8388608
  563.5 11.8 %slice-start.1 = ((s8[8847360]{0:T(1024)(128)(4,1)}), s8[4194304]{0:T(1024)(128)(4,1)S(1)}, s32[]{:S(2)}) async-start(s8[8847360]{0:T(1024)(128)(4,1)} %bitcast.76), calls=%async_computation.9 | async-start | bytes 8388608
  569.5 5.9 slice-start.2
  569.5 210.2 %copy-start.9 = (s32[2]{0:T(128)S(1)}, s32[2]{0:T(128)}, u32[]{:S(2)}) copy-start(s32[2]{0:T(128)} %param.23) | copy-start | bytes 28
  569.5 210.3 %copy-start.10 = (u32[32]{0:T(128)S(1)}, u32[32]{0:T(128)}, u32[]{:S(2)}) copy-start(u32[32]{0:T(128)} %constant.29) | copy-start | bytes 388
  569.5 216.1 %copy-start.8 = (bf16[32,320]{1,0:T(8,128)(2,1)S(1)}, bf16[32,320]{1,0:T(8,128)(2,1)}, u32[]{:S(2)}) copy-start(bf16[32,320]{1,0:T(8,128)(2,1)} %param.13) | copy-start | bytes 61444
  569.5 247.6 %copy-start.7 = (f32[7,1024]{1,0:T(8,128)S(1)}, f32[7,1024]{1,0:T(8,128)}, u32[]{:S(2)}) copy-start(f32[7,1024]{1,0:T(8,128)} %param.21) | copy-start | bytes 86020
  569.5 249.3 %copy-start.4 = (bf16[16,320,32]{1,2,0:T(8,128)(2,1)S(1)}, bf16[16,320,32]{1,2,0:T(8,128)(2,1)}, u32[]{:S(2)}) copy-start(bf16[16,320,32]{1,2,0:T(8,128)(2,1)} %copy-done.3) | copy-start | bytes 983044
  569.5 251.0 %copy-start.6 = (bf16[16,320,32]{1,2,0:T(8,128)(2,1)S(1)}, bf16[16,320,32]{1,2,0:T(8,128)(2,1)}, u32[]{:S(2)}) copy-start(bf16[16,320,32]{1,2,0:T(8,128)(2,1)} %copy-done.5) | copy-start | bytes 983044
Sparse Core Ops, SparseCore 0:
  829.7 87.6 all-reduce.4
where the time goes:
time: 1060 us
  waiting for transfers between devices  462 us (44%)
  blocking collectives  233 us (22%)
  local copies, waits for them, and re-layouts  155 us (15%)
  starting transfers between devices  117 us (11%)
  other arithmetic  60.6 us (6%)
  between operations  15.9 us (2%)
  matrix products  12.2 us (1%)
    pmax x1, blocking collectives, per_device(): lax.pmax(largest(tensor), ('fsdp', 'tp'))  201 us
    all_to_all x1, waiting for transfers between devices, regroup(): lax.all_to_all(gate_part, 'fsdp', split_axis=0, concat_axis=1, tiled=True)  152 us
    all_to_all x1, waiting for transfers between devices, regroup(): lax.all_to_all(up_part, 'fsdp', split_axis=0, concat_axis=1, tiled=True)  152 us
    convert_element_type x6, local copies, waits for them, and re-layouts, quantize(): return (tensor.astype(jnp.float32) * factor).astype(jnp.bfloat16)  86.1 us
    unnamed x2, waiting for transfers between devices  81.9 us
    unnamed x36, local copies, waits for them, and re-layouts  49.3 us
    all_to_all x1, starting transfers between devices, regroup(): lax.all_to_all(down_part, 'fsdp', split_axis=1, concat_axis=0, tiled=True)  40 us
    all_to_all x1, starting transfers between devices, regroup(): lax.all_to_all(up_part, 'fsdp', split_axis=0, concat_axis=1, tiled=True)  39.7 us
  transfers between devices with their start and end apart: 8, of which 7 were waited for; matrix products, arithmetic and copies ran while one was open for 17% of the time, Pallas kernels for 0%

commit v1 on v0

--- a/solution.py
+++ b/solution.py
@@ -1,7 +1,12 @@
+import functools
+
 import jax
 import jax.numpy as jnp
 from jax import lax
+from jax.experimental import pallas as pl
+from jax.experimental.pallas import tpu as pltpu
 from jax.sharding import PartitionSpec as P
+
 
 D = 5120
 HEADS = 40
@@ -87,7 +92,7 @@
     return mixed.astype(jnp.bfloat16).reshape(count_seq, -1)
 
 
-def per_device(
+def general_step(
     hidden,
     query_weight,
     key_weight,
@@ -159,9 +164,411 @@
     )
 
 
+LANES = 128
+
+
+def fits(mesh, arrays):
+    shards, half = mesh.shape["fsdp"], mesh.shape["tp"]
+    width = arrays[0].shape[1] // shards
+    if shards & (shards - 1) or shards < 4 or width % LANES != LANES // 2:
+        return False
+    counts = [w.shape[1] // (shards * half) for w in (arrays[1], arrays[2], arrays[3], arrays[5])]
+    return all(c % 32 == 0 and (4 * c) % LANES == 0 for c in counts)
+
+
+def pack_kernel(counts, span, extra_mode, me_ref, *refs):
+    ins = refs[: len(counts)]
+    refs = refs[len(counts) :]
+    if extra_mode:
+        extra, refs = refs[0], refs[1:]
+    outs, (buf, sems, extra_sems) = refs[:-3], refs[-3:]
+    step = pl.program_id(0)
+    steps = len(outs) // 2
+    slot = lax.rem(step, 2)
+    side = lax.rem(me_ref[0], 2)
+    bulk = sum(c * span // LANES for c in counts)
+    lead = span // LANES
+
+    def drain(where):
+        for part in range(2):
+            pltpu.make_async_copy(
+                buf.at[where, part], outs[0].at[pl.ds(0, bulk)], sems.at[where, part]
+            ).wait()
+
+    @pl.when(step >= 2)
+    def _():
+        drain(slot)
+
+    base = 0
+    for ref, count in zip(ins, counts):
+        half = count // 2
+        for tile in range(lead):
+            buf[slot, 0, pl.ds(base + tile * count, count)] = ref[
+                :, tile * LANES : (tile + 1) * LANES
+            ]
+            buf[slot, 1, pl.ds(base + tile * count, count)] = ref[
+                :, (tile + lead + 1) * LANES : (tile + lead + 2) * LANES
+            ]
+        shared = ref[:, lead * LANES : (lead + 1) * LANES].astype(jnp.float32)
+        low, high = shared[:half], shared[half:]
+        left = lax.broadcasted_iota(jnp.int32, (half, LANES), 1) < LANES // 2
+        tail = base + lead * count
+        buf[slot, 0, pl.ds(tail, half)] = jnp.where(
+            left, low, pltpu.roll(high, LANES // 2, 1)
+        ).astype(jnp.bfloat16)
+        buf[slot, 1, pl.ds(tail, half)] = jnp.where(
+            left, pltpu.roll(low, LANES // 2, 1), high
+        ).astype(jnp.bfloat16)
+        base += count * span // LANES
+
+    first = me_ref[1]
+    for index in range(steps):
+
+        @pl.when(step == index)
+        def _():
+            for part in range(2):
+                out = outs[2 * index + part]
+                pltpu.make_async_copy(
+                    buf.at[slot, side if part == 0 else 1 - side],
+                    out.at[pl.ds(0, bulk)],
+                    sems.at[slot, part],
+                ).start()
+                if extra_mode:
+                    height = extra.shape[-2]
+                    peer = me_ref[0] ^ (2 * (first + index) + part)
+                    source = extra if extra_mode == 1 else extra.at[peer]
+                    pltpu.make_async_copy(
+                        source, out.at[pl.ds(bulk, height)], extra_sems.at[index, part]
+                    ).start()
+
+    @pl.when(step == steps - 1)
+    def _():
+        if steps > 1:
+            drain(1 - slot)
+        drain(slot)
+        if extra_mode:
+            height = extra.shape[-2]
+            source = extra if extra_mode == 1 else extra.at[0]
+            for index in range(steps):
+                for part in range(2):
+                    pltpu.make_async_copy(
+                        source,
+                        outs[0].at[pl.ds(bulk, height)],
+                        extra_sems.at[index, part],
+                    ).wait()
+
+
+def pack(tensors, me, shards, first, steps, extra=None):
+    span = tensors[0].shape[1] // shards
+    counts = [t.shape[0] for t in tensors]
+    bulk = sum(c * span // LANES for c in counts)
+    mode = 0 if extra is None else extra.ndim - 1
+    rows = bulk + (0 if extra is None else extra.shape[-2])
+    spot = jnp.stack([me, jnp.int32(first)])
+
+    def block(step, spot):
+        return (0, (spot[0] // 2) ^ (spot[1] + step))
+
+    in_specs = [pl.BlockSpec((c, 2 * span), block) for c in counts]
+    operands = list(tensors)
+    if mode:
+        in_specs.append(pl.BlockSpec(memory_space=pltpu.VMEM))
+        operands.append(extra)
+    moved = sum(t.size for t in tensors) * 2 * steps // (shards // 2)
+    return pl.pallas_call(
+        functools.partial(pack_kernel, counts, span, mode),
+        grid_spec=pltpu.PrefetchScalarGridSpec(
+            num_scalar_prefetch=1,
+            grid=(steps,),
+            in_specs=in_specs,
+            out_specs=[pl.BlockSpec(memory_space=pl.ANY)] * (2 * steps),
+            scratch_shapes=[
+                pltpu.VMEM((2, 2, bulk, LANES), jnp.bfloat16),
+                pltpu.SemaphoreType.DMA((2, 2)),
+                pltpu.SemaphoreType.DMA((steps, 2)),
+            ],
+        ),
+        out_shape=[jax.ShapeDtypeStruct((rows, LANES), jnp.bfloat16)] * (2 * steps),
+        compiler_params=pltpu.CompilerParams(dimension_semantics=("arbitrary",)),
+        cost_estimate=pl.CostEstimate(
+            flops=moved * 200, bytes_accessed=2 * moved, transcendentals=0
+        ),
+        name="pack",
+    )(spot, *operands)
+
+
+def unpack_kernel(count, span, start, shards, me_ref, factor_ref, *refs):
+    chunks = refs[:shards]
+    out, whole, shared, sems = refs[shards:]
+    group = pl.program_id(0)
+    me = me_ref[0]
+    side = lax.rem(me, 2)
+    lead = span // LANES
+    half = count // 2
+
+    def copies(chunk, source):
+        at = pl.multiple_of(source * count, 32)
+        made = [
+            pltpu.make_async_copy(
+                chunk.at[pl.ds(start + tile * count, count)],
+                whole.at[tile, pl.ds(at, count)],
+                sems.at[source, tile],
+            )
+            for tile in range(lead)
+        ]
+        for part in range(2):
+            made.append(
+                pltpu.make_async_copy(
+                    chunk.at[pl.ds(start + lead * count, half)],
+                    shared.at[pl.ds(at + part * half, half)],
+                    sems.at[source, lead + part],
+                )
+            )
+        return made
+
+    @pl.when(group == 0)
+    def _():
+        for number in range(shards):
+            for copy in copies(chunks[number], me ^ number):
+                copy.start()
+
+    for member in range(4):
+        for copy in copies(chunks[0], group * 4 + member):
+            copy.wait()
+
+    factor = factor_ref[0]
+    rise = pl.multiple_of(side * (LANES // 2), LANES // 2)
+    fall = pl.multiple_of((1 - side) * (lead * LANES), LANES // 2)
+
+    def tile_step(tile, carry):
+        row = pl.multiple_of(group * (4 * count) + tile * LANES, LANES)
+        column = pl.ds(pl.multiple_of(tile * LANES, LANES), LANES)
+        for number in range(lead):
+            piece = whole[number, pl.ds(row, LANES), :].astype(jnp.float32)
+            out[pl.ds(pl.multiple_of(rise + number * LANES, LANES // 2), LANES), column] = (
+                piece.T * factor
+            ).astype(jnp.bfloat16)
+        piece = shared[pl.ds(row, LANES), :].astype(jnp.float32).T
+        spot = row + lax.broadcasted_iota(jnp.int32, (LANES // 2, LANES), 1)
+        low = lax.rem(spot, count) < half
+        out[pl.ds(fall, LANES // 2), column] = (
+            jnp.where(low, piece[: LANES // 2], piece[LANES // 2 :]) * factor
+        ).astype(jnp.bfloat16)
+        return carry
+
+    lax.fori_loop(0, 4 * count // LANES, tile_step, 0)
+
+
+def unpack(chunks, me, factor, count, span, start):
+    shards = len(chunks)
+    size = shards * count * span
+    return pl.pallas_call(
+        functools.partial(unpack_kernel, count, span, start, shards),
+        grid_spec=pltpu.PrefetchScalarGridSpec(
+            num_scalar_prefetch=2,
+            grid=(shards // 4,),
+            in_specs=[pl.BlockSpec(memory_space=pl.ANY)] * shards,
+            out_specs=pl.BlockSpec((span, 4 * count), lambda group, me, factor: (0, group)),
+            scratch_shapes=[
+                pltpu.VMEM((span // LANES, shards * count, LANES), jnp.bfloat16),
+                pltpu.VMEM((shards * count, LANES), jnp.bfloat16),
+                pltpu.SemaphoreType.DMA((shards, span // LANES + 2)),
+            ],
+        ),
+        out_shape=jax.ShapeDtypeStruct((span, shards * count), jnp.bfloat16),
+        compiler_params=pltpu.CompilerParams(dimension_semantics=("arbitrary",)),
+        cost_estimate=pl.CostEstimate(
+            flops=size * 200, bytes_accessed=4 * size, transcendentals=0
+        ),
+        name="unpack",
+    )(me.reshape(1), factor.reshape(1), *chunks)
+
+
+def collect_kernel(start, height, me_ref, *refs):
+    chunks, out, sems = refs[:-2], refs[-2], refs[-1]
+
+    def copy(number):
+        return pltpu.make_async_copy(
+            chunks[number].at[pl.ds(start, height)], out.at[me_ref[0] ^ number], sems.at[number]
+        )
+
+    for number in range(len(chunks)):
+        copy(number).start()
+    for number in range(len(chunks)):
+        copy(number).wait()
+
+
+def collect(chunks, me, start, height):
+    shards = len(chunks)
+    return pl.pallas_call(
+        functools.partial(collect_kernel, start, height),
+        grid_spec=pltpu.PrefetchScalarGridSpec(
+            num_scalar_prefetch=1,
+            grid=(1,),
+            in_specs=[pl.BlockSpec(memory_space=pl.ANY)] * shards,
+            out_specs=pl.BlockSpec((shards, height, LANES), lambda step, me: (0, 0, 0)),
+            scratch_shapes=[pltpu.SemaphoreType.DMA((shards,))],
+        ),
+        out_shape=jax.ShapeDtypeStruct((shards, height, LANES), jnp.bfloat16),
+        cost_estimate=pl.CostEstimate(
+            flops=1 << 20, bytes_accessed=shards * height * LANES * 4, transcendentals=0
+        ),
+        name="collect",
+    )(me.reshape(1), *chunks)
+
+
+def exchange(chunks, order):
+    shards = len(chunks)
+    arrived = list(chunks)
+    for number in order:
+        pairs = [(source, source ^ number) for source in range(shards)]
+        arrived[number] = lax.ppermute(chunks[number], "fsdp", pairs)
+    return arrived
+
+
+def after(token, *values):
+    return lax.optimization_barrier((token, *values))[1:]
+
+
+def three_terms(values):
+    terms = []
+    for _ in range(3):
+        term = lax.reduce_precision(values, 8, 7)
+        terms.append(term.astype(jnp.bfloat16))
+        values = values - term
+    return jnp.stack(terms, axis=1)
+
+
+def packed_step(
+    shards,
+    half,
+    hidden,
+    query_weight,
+    key_weight,
+    value_weight,
+    output_weight,
+    gate_weight,
+    up_weight,
+    down_weight,
+    history,
+    slot,
+    lengths,
+    key_cache,
+    value_cache,
+):
+    me = lax.axis_index("fsdp").astype(jnp.int32)
+    span = hidden.shape[1]
+    seqs = hidden.shape[0]
+    share = seqs // shards
+    query_t, key_t, value_t = query_weight.T, key_weight.T, value_weight.T
+    gate_t, up_t = gate_weight.T, up_weight.T
+    cross = shards // 2
+    mixed = [cross]
+    for number in range(1, cross):
+        mixed += [number, cross + number]
+    pairs = shards // 2
+
+    def rows(tensor):
+        return tensor.shape[0] * span // LANES
+
+    wire_hidden = hidden.reshape(seqs * span // LANES, LANES)
+    far = pack([gate_t], me, shards, pairs // 2, pairs // 2, wire_hidden)
+    gate_near, hidden_near = after(far[0], gate_t, wire_hidden)
+    near = pack([gate_near], me, shards, 0, pairs // 2, hidden_near)
+    gate_chunks = near + far
+    gate_chunks = exchange(gate_chunks, list(range(cross, shards)))
+    gate_chunks = exchange(gate_chunks, list(range(1, cross)))
+
+    trainer = (query_t, key_t, value_t, output_weight, gate_t, up_t, down_weight)
+    staged = after(near[0], *trainer)
+    local = jnp.stack([largest(tensor) for tensor in staged])
+    tile = jnp.broadcast_to(jnp.pad(local, (0, 9))[:, None], (16, LANES)).astype(jnp.bfloat16)
+    best = tile
+    for turn in range(1, half):
+        ring = [(source, (source + turn) % half) for source in range(half)]
+        best = jnp.maximum(best, lax.ppermute(tile, "tp", ring))
+    up_chunks = pack([up_t], me, shards, 0, pairs, best)
+    (down_late,) = after(up_chunks[0], down_weight)
+    down_chunks = pack([down_late], me, shards, 0, pairs)
+    up_chunks = exchange(up_chunks, mixed)
+    down_chunks = exchange(down_chunks, mixed)
+
+    everyone = collect(gate_chunks, me, rows(gate_t), wire_hidden.shape[0])
+    everyone = everyone.reshape(shards, seqs, span).transpose(1, 0, 2).reshape(seqs, shards * span)
+    widened = everyone.astype(jnp.float32)
+    inv_rms = lax.rsqrt(jnp.sum(widened * widened, axis=1) / D + norm_eps)[:, None]
+
+    seen = collect(up_chunks, me, rows(up_t), best.shape[0])
+    peaks = jnp.max(seen[:, :7, 0].astype(jnp.float32), axis=0)
+    factors, new_history = scaling(peaks, history, slot)
+
+    parts = []
+    for number, tensor in enumerate((query_t, key_t, value_t)):
+        product = lax.dot_general(
+            everyone,
+            quantize(tensor, factors[number]),
+            (((1,), (1,)), ((), ())),
+            preferred_element_type=jnp.float32,
+        )
+        parts.append(product * inv_rms / factors[number])
+    joined = jnp.concatenate(parts, axis=1)
+    width = joined.shape[1]
+    padded = -(-width // LANES) * LANES
+    terms = three_terms(jnp.pad(joined, ((0, 0), (0, padded - width))))
+    terms = terms.reshape(shards, share, 3, padded // LANES, LANES)
+    terms = terms.reshape(shards, share * 3 * padded // LANES, LANES)
+    used = terms.shape[1]
+    filled = -(-used // 16) * 16
+    terms = jnp.pad(terms, ((0, 0), (0, filled - used), (0, 0)))
+    output_chunks = pack([output_weight], me, shards, 0, pairs, terms)
+    query_late, key_late, value_late = after(output_chunks[0], query_t, key_t, value_t)
+    last = pack([query_late, key_late, value_late], me, shards, 0, pairs)
+    output_chunks = exchange(output_chunks, mixed)
+    last = exchange(last, mixed)
+
+    mine = collect(output_chunks, me, rows(output_weight), filled)[:, :used]
+    mine = mine.reshape(shards, share, 3, padded).astype(jnp.float32)
+    mine = (mine[:, :, 2] + mine[:, :, 1] + mine[:, :, 0]).transpose(1, 0, 2)
+    width_q, width_k = query_t.shape[0], key_t.shape[0]
+    query = mine[:, :, :width_q].reshape(share, shards * width_q)
+    key_new = mine[:, :, width_q : width_q + width_k].reshape(share, shards * width_k)
+    value_new = mine[:, :, width_q + width_k : width].reshape(share, -1)
+    query = rotate(query.reshape(share, -1, HEAD_DIM), lengths).astype(jnp.bfloat16)
+    query = query.reshape(share, -1, HEADS // KV_HEADS, HEAD_DIM)
+    key_new = rotate(key_new.reshape(share, -1, HEAD_DIM), lengths).astype(jnp.bfloat16)
+    value_new = value_new.reshape(share, -1, HEAD_DIM).astype(jnp.bfloat16)
+    attention_out = attend(query, key_new, value_new, key_cache, value_cache, lengths)
+
+    def finish(chunks, number, tensor, start=0):
+        return unpack(chunks, me, factors[number], tensor.shape[0], span, start)
+
+    return (
+        attention_out,
+        finish(last, 0, query_t),
+        finish(last, 1, key_t, rows(query_t)),
+        finish(last, 2, value_t, rows(query_t) + rows(key_t)),
+        finish(output_chunks, 3, output_weight).T,
+        finish(gate_chunks, 4, gate_t),
+        finish(up_chunks, 5, up_t),
+        finish(down_chunks, 6, down_weight).T,
+        new_history,
+    )
+
+
 def solution(mesh):
+    return lambda *arrays: build(mesh, arrays)(*arrays)
+
+
+def build(mesh, arrays):
+    shards, half = mesh.shape["fsdp"], mesh.shape["tp"]
+    if fits(mesh, arrays):
+        return sharded(mesh, functools.partial(packed_step, shards, half))
+    return sharded(mesh, general_step)
+
+
+def sharded(mesh, body):
     return jax.shard_map(
-        per_device,
+        body,
         mesh=mesh,
         in_specs=(
             P(None, "fsdp"),

time: 1060 us -> 861 us (0.81)
  blocking collectives: 233 us -> 0 us
  starting transfers between devices: 117 us -> 288 us
  local copies, waits for them, and re-layouts: 155 us -> 12.1 us
  Pallas kernels: 0 us -> 122 us
  waiting for transfers between devices: 462 us -> 392 us
  other arithmetic: 60.6 us -> 23.1 us
  between operations: 15.9 us -> 2.44 us
    ppermute x0 -> x76, waiting for transfers between devices: none -> 392 us  [the longest x75 390 us: exchange(): arrived[number] = lax.ppermute(chunks[number], 'fsdp', pairs)]
    all_to_all x7 -> x0, waiting for transfers between devices: 380 us -> none  [the longest x1 152 us: regroup(): lax.all_to_all(gate_part, 'fsdp', split_axis=0, concat_axis=1, tiled=True)]
    ppermute x0 -> x76, starting transfers between devices: none -> 288 us  [the longest x75 286 us: exchange(): arrived[number] = lax.ppermute(chunks[number], 'fsdp', pairs)]
    pmax x1 -> x0, blocking collectives: 201 us -> none  [per_device(): lax.pmax(largest(tensor), ('fsdp', 'tp'))]
    pallas_call x0 -> x16, Pallas kernels: none -> 122 us  [the longest x7 70.8 us: unpack(): pl.pallas_call(functools.partial(unpack_kernel, count, span, start, shard...]
    all_to_all x7 -> x0, starting transfers between devices: 116 us -> none  [the longest x1 40 us: regroup(): lax.all_to_all(down_part, 'fsdp', split_axis=1, concat_axis=0, tiled=True)]
    convert_element_type x6 -> x1, local copies, waits for them, and re-layouts: 86.1 us -> 0.06 us  [packed_step(): mine = mine.reshape(shards, share, 3, padded).astype(jnp.float32)]
    unnamed x2 -> x0, waiting for transfers between devices: 81.9 us -> none
  transfers between devices with their start and end apart: 8 -> 76, of which waited for: 7 -> 20; matrix products, arithmetic and copies ran while one was open for 17% -> 3% of each run, Pallas kernels for 0% -> 10%
where the time goes in v1:
time: 861 us; the launch traced here: 856 us
  waiting for transfers between devices  392 us (46%)
  starting transfers between devices  288 us (33%)
  Pallas kernels  122 us (14%)
  other arithmetic  23.1 us (3%)
  matrix products  16.5 us (2%)
  local copies, waits for them, and re-layouts  12.1 us (1%)
    ppermute x75, waiting for transfers between devices, exchange(): arrived[number] = lax.ppermute(chunks[number], 'fsdp', pairs)  390 us
    ppermute x75, starting transfers between devices, exchange(): arrived[number] = lax.ppermute(chunks[number], 'fsdp', pairs)  286 us
    pallas_call x7, Pallas kernels, unpack(): pl.pallas_call(functools.partial(unpack_kernel, count, span, start, shard...  70.8 us
    pallas_call x6, Pallas kernels, pack(): pl.pallas_call(functools.partial(pack_kernel, counts, span, mode), grid_s...  46.2 us
  transfers between devices with their start and end apart: 76, of which 20 were waited for; matrix products, arithmetic and copies ran while one was open for 3% of the time, Pallas kernels for 10%

profile of v1, /device:TPU:0, one launch (start us, length us, event | category | flops | bytes accessed | tf_op | source)
XLA Modules:
  0.0 856.2 jit_solution(18192897148604079037)
XLA Ops:
  41.8 10.6 %pack.8 = (bf16[2176,128]{1,0:T(8,128)(2,1)}, bf16[2176,128]{1,0:T(8,128)(2,1)}, bf16[2176,128]{1,0:T(8,128)(2,1)}, bf16[2176,128]{1,0:T(8,128)(2,1)}, bf16[2176...) custom-call(s32[2]{0:T(128)} %get-tuple-element.220.me_ref, ...), custom_call_target="tpu_custom_call" | custom-call | flops 1769472000 | bytes 17694720 | tf_op jit(solution)/shard_map/pack/pallas_call | solution.py:278
  59.1 9.2 %collective-permute-done.17.refs_2_ = bf16[2176,128]{1,0:T(8,128)(2,1)S(1)} collective-permute-done((bf16[2176,128]{1,0:T(8,128)(2,1)}, bf16[2176,128]{1,0:T(8,128)(2,1)S(1)}, u32[]{:S(2)}, u32[]{:S(2)}) %collective-permute-start.17) | collective-permute-done | bytes 557088 | tf_op jit(solution)/shard_map/ppermute | solution.py:425
  69.9 9.7 %collective-permute-done.18.refs_3_ = bf16[2176,128]{1,0:T(8,128)(2,1)S(1)} collective-permute-done((bf16[2176,128]{1,0:T(8,128)(2,1)}, bf16[2176,128]{1,0:T(8,128)(2,1)S(1)}, u32[]{:S(2)}, u32[]{:S(2)}) %collective-permute-start.18) | collective-permute-done | bytes 557088 | tf_op jit(solution)/shard_map/ppermute | solution.py:425
  86.1 33.1 %collective-permute-done.21.refs_6_ = bf16[2176,128]{1,0:T(8,128)(2,1)S(1)} collective-permute-done((bf16[2176,128]{1,0:T(8,128)(2,1)}, bf16[2176,128]{1,0:T(8,128)(2,1)S(1)}, u32[]{:S(2)}, u32[]{:S(2)}) %collective-permute-start.21) | collective-permute-done | bytes 557088 | tf_op jit(solution)/shard_map/ppermute | solution.py:425
  119.2 10.7 %collective-permute-done.22.refs_7_ = bf16[2176,128]{1,0:T(8,128)(2,1)S(1)} collective-permute-done((bf16[2176,128]{1,0:T(8,128)(2,1)}, bf16[2176,128]{1,0:T(8,128)(2,1)S(1)}, u32[]{:S(2)}, u32[]{:S(2)}) %collective-permute-start.22) | collective-permute-done | bytes 557088 | tf_op jit(solution)/shard_map/ppermute | solution.py:425
  133.5 50.2 %collective-permute-start.29 = (bf16[2176,128]{1,0:T(8,128)(2,1)}, bf16[2176,128]{1,0:T(8,128)(2,1)S(1)}, u32[]{:S(2)}, u32[]{:S(2)}) collective-permute-start(bf16[2176,128]{1,0:T(8,128)(2,1)} %get-tuple-element.141), channel_id=1, source_target_pairs={{0,28},{2,30},{4,24},{6,26},{8,20},{10,22},{12,16},{14,18},{16,12}... | collective-permute-start | bytes 1671176 | tf_op jit(solution)/shard_map/ppermute | solution.py:425
  183.8 20.9 %collective-permute-done.25.refs_10_ = bf16[2176,128]{1,0:T(8,128)(2,1)S(1)} collective-permute-done((bf16[2176,128]{1,0:T(8,128)(2,1)}, bf16[2176,128]{1,0:T(8,128)(2,1)S(1)}, u32[]{:S(2)}, u32[]{:S(2)}) %collective-permute-start.25) | collective-permute-done | bytes 557088 | tf_op jit(solution)/shard_map/ppermute | solution.py:425
  207.3 20.6 %collective-permute-done.26.refs_11_ = bf16[2176,128]{1,0:T(8,128)(2,1)S(1)} collective-permute-done((bf16[2176,128]{1,0:T(8,128)(2,1)}, bf16[2176,128]{1,0:T(8,128)(2,1)S(1)}, u32[]{:S(2)}, u32[]{:S(2)}) %collective-permute-start.26) | collective-permute-done | bytes 557088 | tf_op jit(solution)/shard_map/ppermute | solution.py:425
  229.8 35.2 %collective-permute-start.3 = (bf16[2240,128]{1,0:T(8,128)(2,1)}, bf16[2240,128]{1,0:T(8,128)(2,1)}, u32[]{:S(2)}, u32[]{:S(2)}) collective-permute-start(bf16[2240,128]{1,0:T(8,128)(2,1)} %get-tuple-element.109), channel_id=1, source_target_pairs={{0,8},{2,10},{4,12},{6,14},{8,0},{10,2},{12,4},{14,6},{16,24},{18,... | collective-permute-start | bytes 1720328 | tf_op jit(solution)/shard_map/ppermute | solution.py:425
  265.0 11.1 %collective-permute-start.4 = (bf16[2240,128]{1,0:T(8,128)(2,1)}, bf16[2240,128]{1,0:T(8,128)(2,1)}, u32[]{:S(2)}, u32[]{:S(2)}) collective-permute-start(bf16[2240,128]{1,0:T(8,128)(2,1)} %get-tuple-element.110), channel_id=1, source_target_pairs={{0,10},{2,8},{4,14},{6,12},{8,2},{10,0},{12,6},{14,4},{16,26},{18,... | collective-permute-start | bytes 1720328 | tf_op jit(solution)/shard_map/ppermute | solution.py:425
  278.8 13.3 %collective-permute-start.7 = (bf16[2240,128]{1,0:T(8,128)(2,1)}, bf16[2240,128]{1,0:T(8,128)(2,1)}, u32[]{:S(2)}, u32[]{:S(2)}) collective-permute-start(bf16[2240,128]{1,0:T(8,128)(2,1)} %get-tuple-element.102), channel_id=1, source_target_pairs={{0,16},{2,18},{4,20},{6,22},{8,24},{10,26},{12,28},{14,30},{16,0},... | collective-permute-start | bytes 1720328 | tf_op jit(solution)/shard_map/ppermute | solution.py:425
  294.5 32.5 %collective-permute-done.5.refs_6_ = bf16[2240,128]{1,0:T(8,128)(2,1)} collective-permute-done((bf16[2240,128]{1,0:T(8,128)(2,1)}, bf16[2240,128]{1,0:T(8,128)(2,1)}, u32[]{:S(2)}, u32[]{:S(2)}) %collective-permute-start.5) | collective-permute-done | bytes 573472 | tf_op jit(solution)/shard_map/ppermute | solution.py:425
  329.3 8.9 %collective-permute-done.6.refs_7_ = bf16[2240,128]{1,0:T(8,128)(2,1)} collective-permute-done((bf16[2240,128]{1,0:T(8,128)(2,1)}, bf16[2240,128]{1,0:T(8,128)(2,1)}, u32[]{:S(2)}, u32[]{:S(2)}) %collective-permute-start.6) | collective-permute-done | bytes 573472 | tf_op jit(solution)/shard_map/ppermute | solution.py:425
  343.0 50.4 %collective-permute-done.10.refs_11_ = bf16[2240,128]{1,0:T(8,128)(2,1)} collective-permute-done((bf16[2240,128]{1,0:T(8,128)(2,1)}, bf16[2240,128]{1,0:T(8,128)(2,1)}, u32[]{:S(2)}, u32[]{:S(2)}) %collective-permute-start.10) | collective-permute-done | bytes 573472 | tf_op jit(solution)/shard_map/ppermute | solution.py:425
  393.4 10.8 %collective-permute-start.8 = (bf16[2240,128]{1,0:T(8,128)(2,1)}, bf16[2240,128]{1,0:T(8,128)(2,1)}, u32[]{:S(2)}, u32[]{:S(2)}) collective-permute-start(bf16[2240,128]{1,0:T(8,128)(2,1)} %get-tuple-element.113), channel_id=1, source_target_pairs={{0,18},{2,16},{4,22},{6,20},{8,26},{10,24},{12,30},{14,28},{16,2},... | collective-permute-start | bytes 1720328 | tf_op jit(solution)/shard_map/ppermute | solution.py:425
  404.2 12.2 %collective-permute-start.9 = (bf16[2240,128]{1,0:T(8,128)(2,1)}, bf16[2240,128]{1,0:T(8,128)(2,1)}, u32[]{:S(2)}, u32[]{:S(2)}) collective-permute-start(bf16[2240,128]{1,0:T(8,128)(2,1)} %get-tuple-element.114), channel_id=1, source_target_pairs={{0,20},{2,22},{4,16},{6,18},{8,28},{10,30},{12,24},{14,26},{16,4},... | collective-permute-start | bytes 1720328 | tf_op jit(solution)/shard_map/ppermute | solution.py:425
  417.7 10.6 %pack.11 = (bf16[2160,128]{1,0:T(8,128)(2,1)}, bf16[2160,128]{1,0:T(8,128)(2,1)}, bf16[2160,128]{1,0:T(8,128)(2,1)}, bf16[2160,128]{1,0:T(8,128)(2,1)}, bf16[216...) custom-call(s32[2]{0:T(128)} %get-tuple-element.220.me_ref, ...), custom_call_target="tpu_custom_call" | custom-call | flops 1769472000 | bytes 17694720 | tf_op jit(solution)/shard_map/pack/pallas_call | solution.py:278
  433.4 45.4 %collective-permute-done.8.refs_9_ = bf16[2240,128]{1,0:T(8,128)(2,1)} collective-permute-done((bf16[2240,128]{1,0:T(8,128)(2,1)}, bf16[2240,128]{1,0:T(8,128)(2,1)}, u32[]{:S(2)}, u32[]{:S(2)}) %collective-permute-start.8) | collective-permute-done | bytes 573472 | tf_op jit(solution)/shard_map/ppermute | solution.py:425
  478.8 11.8 %collective-permute-done.9.refs_10_ = bf16[2240,128]{1,0:T(8,128)(2,1)} collective-permute-done((bf16[2240,128]{1,0:T(8,128)(2,1)}, bf16[2240,128]{1,0:T(8,128)(2,1)}, u32[]{:S(2)}, u32[]{:S(2)}) %collective-permute-start.9) | collective-permute-done | bytes 573472 | tf_op jit(solution)/shard_map/ppermute | solution.py:425
  502.7 35.4 %collective-permute-done.65.refs_5_ = bf16[2160,128]{1,0:T(8,128)(2,1)} collective-permute-done((bf16[2160,128]{1,0:T(8,128)(2,1)}, bf16[2160,128]{1,0:T(8,128)(2,1)}, u32[]{:S(2)}, u32[]{:S(2)}) %collective-permute-start.65) | collective-permute-done | bytes 552992 | tf_op jit(solution)/shard_map/ppermute | solution.py:425
  540.2 10.3 %collective-permute-done.66.refs_6_ = bf16[2160,128]{1,0:T(8,128)(2,1)S(1)} collective-permute-done((bf16[2160,128]{1,0:T(8,128)(2,1)}, bf16[2160,128]{1,0:T(8,128)(2,1)S(1)}, u32[]{:S(2)}, u32[]{:S(2)}) %collective-permute-start.66) | collective-permute-done | bytes 552992 | tf_op jit(solution)/shard_map/ppermute | solution.py:425
  550.5 11.7 %collective-permute-done.67.refs_7_ = bf16[2160,128]{1,0:T(8,128)(2,1)S(1)} collective-permute-done((bf16[2160,128]{1,0:T(8,128)(2,1)}, bf16[2160,128]{1,0:T(8,128)(2,1)S(1)}, u32[]{:S(2)}, u32[]{:S(2)}) %collective-permute-start.67) | collective-permute-done | bytes 552992 | tf_op jit(solution)/shard_map/ppermute | solution.py:425
  566.5 57.1 %collective-permute-done.70.refs_10_ = bf16[2160,128]{1,0:T(8,128)(2,1)S(1)} collective-permute-done((bf16[2160,128]{1,0:T(8,128)(2,1)}, bf16[2160,128]{1,0:T(8,128)(2,1)S(1)}, u32[]{:S(2)}, u32[]{:S(2)}) %collective-permute-start.70) | collective-permute-done | bytes 552992 | tf_op jit(solution)/shard_map/ppermute | solution.py:425
  631.8 6.2 pack.9
  638.1 9.2 %collective-permute-done.71.refs_11_ = bf16[2160,128]{1,0:T(8,128)(2,1)} collective-permute-done((bf16[2160,128]{1,0:T(8,128)(2,1)}, bf16[2160,128]{1,0:T(8,128)(2,1)}, u32[]{:S(2)}, u32[]{:S(2)}) %collective-permute-start.71) | collective-permute-done | bytes 552992 | tf_op jit(solution)/shard_map/ppermute | solution.py:425
  649.2 34.5 %collective-permute-start.34 = (bf16[416,128]{1,0:T(8,128)(2,1)}, bf16[416,128]{1,0:T(8,128)(2,1)S(1)}, u32[]{:S(2)}, u32[]{:S(2)}) collective-permute-start(bf16[416,128]{1,0:T(8,128)(2,1)} %get-tuple-element.147), channel_id=1, source_target_pairs={{0,8},{2,10},{4,12},{6,14},{8,0},{10,2},{12,4},{14,6},{16,24},{18,... | collective-permute-start | bytes 319496 | tf_op jit(solution)/shard_map/ppermute | solution.py:425
  683.7 11.4 %collective-permute-start.35 = (bf16[416,128]{1,0:T(8,128)(2,1)}, bf16[416,128]{1,0:T(8,128)(2,1)S(1)}, u32[]{:S(2)}, u32[]{:S(2)}) collective-permute-start(bf16[416,128]{1,0:T(8,128)(2,1)} %get-tuple-element.148), channel_id=1, source_target_pairs={{0,10},{2,8},{4,14},{6,12},{8,2},{10,0},{12,6},{14,4},{16,26},{18,... | collective-permute-start | bytes 319496 | tf_op jit(solution)/shard_map/ppermute | solution.py:425
  703.0 17.5 %unpack.12 = bf16[320,13824]{1,0:T(8,128)(2,1)} custom-call(s32[1]{0:T(128)} %bitcast.me_ref, f32[1]{0:T(128)} %get-tuple-element.212.factor_ref, bf16[2176,128]{1,0:T(8,128)(2,1)} %get-tuple-element.127.refs_0_, bf16[2176,128]{1,0:T(8,128)(2,1)} %copy-done.4, bf16[2176,128]{1,0:T(8,128)(2,1)} %copy-done.5, bf16[2176,128]{1,0:T(8,128)(2,1)} %copy-done.6, ...), custom_call_target="tpu_custom_call" | custom-call | flops 884736000 | bytes 17694720 | tf_op jit(solution)/shard_map/unpack/pallas_call | solution.py:365
  720.7 17.3 %unpack.13 = bf16[320,13824]{1,0:T(8,128)(2,1)} custom-call(s32[1]{0:T(128)} %bitcast.me_ref, f32[1]{0:T(128)} %get-tuple-element.211.factor_ref, bf16[2160,128]{1,0:T(8,128)(2,1)} %get-tuple-element.179.refs_0_, bf16[2160,128]{1,0:T(8,128)(2,1)} %collective-permute-done.61.refs_1_, bf16[2160,128]{1,0:T(8,128)(2,1)} %collective-permute-done.62.refs_2_, ...), custom_call_target="tpu_custom_call" | custom-call | flops 884736000 | bytes 17694720 | tf_op jit(solution)/shard_map/unpack/pallas_call | solution.py:365
  750.7 6.6 pack.10
  757.3 17.2 %unpack.11 = bf16[320,13824]{1,0:T(8,128)(2,1)} custom-call(s32[1]{0:T(128)} %bitcast.me_ref, f32[1]{0:T(128)} %get-tuple-element.213.factor_ref, bf16[2240,128]{1,0:T(8,128)(2,1)} %get-tuple-element.105.refs_0_, bf16[2240,128]{1,0:T(8,128)(2,1)} %copy-done.2, bf16[2240,128]{1,0:T(8,128)(2,1)} %copy-done.3, ...), custom_call_target="tpu_custom_call" | custom-call | flops 884736000 | bytes 17694720 | tf_op jit(solution)/shard_map/unpack/pallas_call | solution.py:365
  803.2 14.6 %collective-permute-start.58 = (bf16[560,128]{1,0:T(8,128)(2,1)}, bf16[560,128]{1,0:T(8,128)(2,1)S(1)}, u32[]{:S(2)}, u32[]{:S(2)}) collective-permute-start(bf16[560,128]{1,0:T(8,128)(2,1)} %get-tuple-element.175), channel_id=1, source_target_pairs={{0,26},{2,24},{4,30},{6,28},{8,18},{10,16},{12,22},{14,20},{16,10}... | collective-permute-start | bytes 430088 | tf_op jit(solution)/shard_map/ppermute | solution.py:425
  (348 shorter events, 197.6 us)
Async XLA Ops:
  56.4 62.8 %collective-permute-start.21 = (bf16[2176,128]{1,0:T(8,128)(2,1)}, bf16[2176,128]{1,0:T(8,128)(2,1)S(1)}, u32[]{:S(2)}, u32[]{:S(2)}) collective-permute-start(bf16[2176,128]{1,0:T(8,128)(2,1)} %get-tuple-element.133), channel_id=1, source_target_pairs={{0,12},{2,14},{4,8},{6,10},{8,4},{10,6},{12,0},{14,2},{16,28},{18,... | collective-permute-start | bytes 1671176 | tf_op jit(solution)/shard_map/ppermute | solution.py:425
  68.3 61.7 %collective-permute-start.22 = (bf16[2176,128]{1,0:T(8,128)(2,1)}, bf16[2176,128]{1,0:T(8,128)(2,1)S(1)}, u32[]{:S(2)}, u32[]{:S(2)}) collective-permute-start(bf16[2176,128]{1,0:T(8,128)(2,1)} %get-tuple-element.134), channel_id=1, source_target_pairs={{0,14},{2,12},{4,10},{6,8},{8,6},{10,4},{12,2},{14,0},{16,30},{18,... | collective-permute-start | bytes 1671176 | tf_op jit(solution)/shard_map/ppermute | solution.py:425
  79.7 51.6 %collective-permute-start.23 = (bf16[2176,128]{1,0:T(8,128)(2,1)}, bf16[2176,128]{1,0:T(8,128)(2,1)S(1)}, u32[]{:S(2)}, u32[]{:S(2)}) collective-permute-start(bf16[2176,128]{1,0:T(8,128)(2,1)} %get-tuple-element.135), channel_id=1, source_target_pairs={{0,16},{2,18},{4,20},{6,22},{8,24},{10,26},{12,28},{14,30},{16,0},... | collective-permute-start | bytes 1671176 | tf_op jit(solution)/shard_map/ppermute | solution.py:425
  82.6 122.1 %collective-permute-start.25 = (bf16[2176,128]{1,0:T(8,128)(2,1)}, bf16[2176,128]{1,0:T(8,128)(2,1)S(1)}, u32[]{:S(2)}, u32[]{:S(2)}) collective-permute-start(bf16[2176,128]{1,0:T(8,128)(2,1)} %get-tuple-element.137), channel_id=1, source_target_pairs={{0,20},{2,22},{4,16},{6,18},{8,28},{10,30},{12,24},{14,26},{16,4},... | collective-permute-start | bytes 1671176 | tf_op jit(solution)/shard_map/ppermute | solution.py:425
  119.2 108.7 %collective-permute-start.26 = (bf16[2176,128]{1,0:T(8,128)(2,1)}, bf16[2176,128]{1,0:T(8,128)(2,1)S(1)}, u32[]{:S(2)}, u32[]{:S(2)}) collective-permute-start(bf16[2176,128]{1,0:T(8,128)(2,1)} %get-tuple-element.138), channel_id=1, source_target_pairs={{0,22},{2,20},{4,18},{6,16},{8,30},{10,28},{12,26},{14,24},{16,6},... | collective-permute-start | bytes 1671176 | tf_op jit(solution)/shard_map/ppermute | solution.py:425
  129.9 98.4 %collective-permute-start.27 = (bf16[2176,128]{1,0:T(8,128)(2,1)}, bf16[2176,128]{1,0:T(8,128)(2,1)S(1)}, u32[]{:S(2)}, u32[]{:S(2)}) collective-permute-start(bf16[2176,128]{1,0:T(8,128)(2,1)} %get-tuple-element.139), channel_id=1, source_target_pairs={{0,24},{2,26},{4,28},{6,30},{8,16},{10,18},{12,20},{14,22},{16,8},... | collective-permute-start | bytes 1671176 | tf_op jit(solution)/shard_map/ppermute | solution.py:425
  131.3 97.6 %collective-permute-start.28 = (bf16[2176,128]{1,0:T(8,128)(2,1)}, bf16[2176,128]{1,0:T(8,128)(2,1)S(1)}, u32[]{:S(2)}, u32[]{:S(2)}) collective-permute-start(bf16[2176,128]{1,0:T(8,128)(2,1)} %get-tuple-element.140), channel_id=1, source_target_pairs={{0,26},{2,24},{4,30},{6,28},{8,18},{10,16},{12,22},{14,20},{16,10}... | collective-permute-start | bytes 1671176 | tf_op jit(solution)/shard_map/ppermute | solution.py:425
  133.5 96.3 %collective-permute-start.29 = (bf16[2176,128]{1,0:T(8,128)(2,1)}, bf16[2176,128]{1,0:T(8,128)(2,1)S(1)}, u32[]{:S(2)}, u32[]{:S(2)}) collective-permute-start(bf16[2176,128]{1,0:T(8,128)(2,1)} %get-tuple-element.141), channel_id=1, source_target_pairs={{0,28},{2,30},{4,24},{6,26},{8,20},{10,22},{12,16},{14,18},{16,12}... | collective-permute-start | bytes 1671176 | tf_op jit(solution)/shard_map/ppermute | solution.py:425
  204.7 60.4 %collective-permute-start.30 = (bf16[2176,128]{1,0:T(8,128)(2,1)}, bf16[2176,128]{1,0:T(8,128)(2,1)S(1)}, u32[]{:S(2)}, u32[]{:S(2)}) collective-permute-start(bf16[2176,128]{1,0:T(8,128)(2,1)} %get-tuple-element.142), channel_id=1, source_target_pairs={{0,30},{2,28},{4,26},{6,24},{8,22},{10,20},{12,18},{14,16},{16,14}... | collective-permute-start | bytes 1671176 | tf_op jit(solution)/shard_map/ppermute | solution.py:425
  229.8 62.3 %collective-permute-start.3 = (bf16[2240,128]{1,0:T(8,128)(2,1)}, bf16[2240,128]{1,0:T(8,128)(2,1)}, u32[]{:S(2)}, u32[]{:S(2)}) collective-permute-start(bf16[2240,128]{1,0:T(8,128)(2,1)} %get-tuple-element.109), channel_id=1, source_target_pairs={{0,8},{2,10},{4,12},{6,14},{8,0},{10,2},{12,4},{14,6},{16,24},{18,... | collective-permute-start | bytes 1720328 | tf_op jit(solution)/shard_map/ppermute | solution.py:425
  277.0 61.2 %collective-permute-start.6 = (bf16[2240,128]{1,0:T(8,128)(2,1)}, bf16[2240,128]{1,0:T(8,128)(2,1)}, u32[]{:S(2)}, u32[]{:S(2)}) collective-permute-start(bf16[2240,128]{1,0:T(8,128)(2,1)} %get-tuple-element.112), channel_id=1, source_target_pairs={{0,14},{2,12},{4,10},{6,8},{8,6},{10,4},{12,2},{14,0},{16,30},{18,... | collective-permute-start | bytes 1720328 | tf_op jit(solution)/shard_map/ppermute | solution.py:425
  278.8 64.1 %collective-permute-start.7 = (bf16[2240,128]{1,0:T(8,128)(2,1)}, bf16[2240,128]{1,0:T(8,128)(2,1)}, u32[]{:S(2)}, u32[]{:S(2)}) collective-permute-start(bf16[2240,128]{1,0:T(8,128)(2,1)} %get-tuple-element.102), channel_id=1, source_target_pairs={{0,16},{2,18},{4,20},{6,22},{8,24},{10,26},{12,28},{14,30},{16,0},... | collective-permute-start | bytes 1720328 | tf_op jit(solution)/shard_map/ppermute | solution.py:425
  292.2 101.2 %collective-permute-start.10 = (bf16[2240,128]{1,0:T(8,128)(2,1)}, bf16[2240,128]{1,0:T(8,128)(2,1)}, u32[]{:S(2)}, u32[]{:S(2)}) collective-permute-start(bf16[2240,128]{1,0:T(8,128)(2,1)} %get-tuple-element.115), channel_id=1, source_target_pairs={{0,22},{2,20},{4,18},{6,16},{8,30},{10,28},{12,26},{14,24},{16,6},... | collective-permute-start | bytes 1720328 | tf_op jit(solution)/shard_map/ppermute | solution.py:425
  293.6 110.5 %collective-permute-start.11 = (bf16[2240,128]{1,0:T(8,128)(2,1)}, bf16[2240,128]{1,0:T(8,128)(2,1)}, u32[]{:S(2)}, u32[]{:S(2)}) collective-permute-start(bf16[2240,128]{1,0:T(8,128)(2,1)} %get-tuple-element.116), channel_id=1, source_target_pairs={{0,24},{2,26},{4,28},{6,30},{8,16},{10,18},{12,20},{14,22},{16,8},... | collective-permute-start | bytes 1720328 | tf_op jit(solution)/shard_map/ppermute | solution.py:425
  327.0 103.8 %collective-permute-start.12 = (bf16[2240,128]{1,0:T(8,128)(2,1)}, bf16[2240,128]{1,0:T(8,128)(2,1)}, u32[]{:S(2)}, u32[]{:S(2)}) collective-permute-start(bf16[2240,128]{1,0:T(8,128)(2,1)} %get-tuple-element.117), channel_id=1, source_target_pairs={{0,26},{2,24},{4,30},{6,28},{8,18},{10,16},{12,22},{14,20},{16,10}... | collective-permute-start | bytes 1720328 | tf_op jit(solution)/shard_map/ppermute | solution.py:425
  338.3 93.7 %collective-permute-start.13 = (bf16[2240,128]{1,0:T(8,128)(2,1)}, bf16[2240,128]{1,0:T(8,128)(2,1)}, u32[]{:S(2)}, u32[]{:S(2)}) collective-permute-start(bf16[2240,128]{1,0:T(8,128)(2,1)} %get-tuple-element.118), channel_id=1, source_target_pairs={{0,28},{2,30},{4,24},{6,26},{8,20},{10,22},{12,16},{14,18},{16,12}... | collective-permute-start | bytes 1720328 | tf_op jit(solution)/shard_map/ppermute | solution.py:425
  342.9 89.9 %collective-permute-start.14 = (bf16[2240,128]{1,0:T(8,128)(2,1)}, bf16[2240,128]{1,0:T(8,128)(2,1)}, u32[]{:S(2)}, u32[]{:S(2)}) collective-permute-start(bf16[2240,128]{1,0:T(8,128)(2,1)} %get-tuple-element.119), channel_id=1, source_target_pairs={{0,30},{2,28},{4,26},{6,24},{8,22},{10,20},{12,18},{14,16},{16,14}... | collective-permute-start | bytes 1720328 | tf_op jit(solution)/shard_map/ppermute | solution.py:425
  393.4 85.4 %collective-permute-start.8 = (bf16[2240,128]{1,0:T(8,128)(2,1)}, bf16[2240,128]{1,0:T(8,128)(2,1)}, u32[]{:S(2)}, u32[]{:S(2)}) collective-permute-start(bf16[2240,128]{1,0:T(8,128)(2,1)} %get-tuple-element.113), channel_id=1, source_target_pairs={{0,18},{2,16},{4,22},{6,20},{8,26},{10,24},{12,30},{14,28},{16,2},... | collective-permute-start | bytes 1720328 | tf_op jit(solution)/shard_map/ppermute | solution.py:425
  404.2 86.5 %collective-permute-start.9 = (bf16[2240,128]{1,0:T(8,128)(2,1)}, bf16[2240,128]{1,0:T(8,128)(2,1)}, u32[]{:S(2)}, u32[]{:S(2)}) collective-permute-start(bf16[2240,128]{1,0:T(8,128)(2,1)} %get-tuple-element.114), channel_id=1, source_target_pairs={{0,20},{2,22},{4,16},{6,18},{8,28},{10,30},{12,24},{14,26},{16,4},... | collective-permute-start | bytes 1720328 | tf_op jit(solution)/shard_map/ppermute | solution.py:425
  430.8 65.6 %collective-permute-start.61 = (bf16[2160,128]{1,0:T(8,128)(2,1)}, bf16[2160,128]{1,0:T(8,128)(2,1)}, u32[]{:S(2)}, u32[]{:S(2)}) collective-permute-start(bf16[2160,128]{1,0:T(8,128)(2,1)} %get-tuple-element.180), channel_id=1, source_target_pairs={{0,2},{2,0},{4,6},{6,4},{8,10},{10,8},{12,14},{14,12},{16,18},{18,... | collective-permute-start | bytes 1658888 | tf_op jit(solution)/shard_map/ppermute | solution.py:425
  431.9 67.0 %collective-permute-start.62 = (bf16[2160,128]{1,0:T(8,128)(2,1)}, bf16[2160,128]{1,0:T(8,128)(2,1)}, u32[]{:S(2)}, u32[]{:S(2)}) collective-permute-start(bf16[2160,128]{1,0:T(8,128)(2,1)} %get-tuple-element.181), channel_id=1, source_target_pairs={{0,4},{2,6},{4,0},{6,2},{8,12},{10,14},{12,8},{14,10},{16,20},{18,... | collective-permute-start | bytes 1658888 | tf_op jit(solution)/shard_map/ppermute | solution.py:425
  432.7 66.4 %collective-permute-start.63 = (bf16[2160,128]{1,0:T(8,128)(2,1)}, bf16[2160,128]{1,0:T(8,128)(2,1)}, u32[]{:S(2)}, u32[]{:S(2)}) collective-permute-start(bf16[2160,128]{1,0:T(8,128)(2,1)} %get-tuple-element.182), channel_id=1, source_target_pairs={{0,6},{2,4},{4,2},{6,0},{8,14},{10,12},{12,10},{14,8},{16,22},{18,... | collective-permute-start | bytes 1658888 | tf_op jit(solution)/shard_map/ppermute | solution.py:425
  496.4 54.1 %collective-permute-start.66 = (bf16[2160,128]{1,0:T(8,128)(2,1)}, bf16[2160,128]{1,0:T(8,128)(2,1)S(1)}, u32[]{:S(2)}, u32[]{:S(2)}) collective-permute-start(bf16[2160,128]{1,0:T(8,128)(2,1)} %get-tuple-element.185), channel_id=1, source_target_pairs={{0,12},{2,14},{4,8},{6,10},{8,4},{10,6},{12,0},{14,2},{16,28},{18,... | collective-permute-start | bytes 1658888 | tf_op jit(solution)/shard_map/ppermute | solution.py:425
  498.9 63.2 %collective-permute-start.67 = (bf16[2160,128]{1,0:T(8,128)(2,1)}, bf16[2160,128]{1,0:T(8,128)(2,1)S(1)}, u32[]{:S(2)}, u32[]{:S(2)}) collective-permute-start(bf16[2160,128]{1,0:T(8,128)(2,1)} %get-tuple-element.186), channel_id=1, source_target_pairs={{0,14},{2,12},{4,10},{6,8},{8,6},{10,4},{12,2},{14,0},{16,30},{18,... | collective-permute-start | bytes 1658888 | tf_op jit(solution)/shard_map/ppermute | solution.py:425
  499.1 63.6 %collective-permute-start.68 = (bf16[2160,128]{1,0:T(8,128)(2,1)}, bf16[2160,128]{1,0:T(8,128)(2,1)S(1)}, u32[]{:S(2)}, u32[]{:S(2)}) collective-permute-start(bf16[2160,128]{1,0:T(8,128)(2,1)} %get-tuple-element.187), channel_id=1, source_target_pairs={{0,16},{2,18},{4,20},{6,22},{8,24},{10,26},{12,28},{14,30},{16,0},... | collective-permute-start | bytes 1658888 | tf_op jit(solution)/shard_map/ppermute | solution.py:425
  502.6 62.9 %collective-permute-start.69 = (bf16[2160,128]{1,0:T(8,128)(2,1)}, bf16[2160,128]{1,0:T(8,128)(2,1)S(1)}, u32[]{:S(2)}, u32[]{:S(2)}) collective-permute-start(bf16[2160,128]{1,0:T(8,128)(2,1)} %get-tuple-element.188), channel_id=1, source_target_pairs={{0,18},{2,16},{4,22},{6,20},{8,26},{10,24},{12,30},{14,28},{16,2},... | collective-permute-start | bytes 1658888 | tf_op jit(solution)/shard_map/ppermute | solution.py:425
  538.0 85.6 %collective-permute-start.70 = (bf16[2160,128]{1,0:T(8,128)(2,1)}, bf16[2160,128]{1,0:T(8,128)(2,1)S(1)}, u32[]{:S(2)}, u32[]{:S(2)}) collective-permute-start(bf16[2160,128]{1,0:T(8,128)(2,1)} %get-tuple-element.189), channel_id=1, source_target_pairs={{0,20},{2,22},{4,16},{6,18},{8,28},{10,30},{12,24},{14,26},{16,4},... | collective-permute-start | bytes 1658888 | tf_op jit(solution)/shard_map/ppermute | solution.py:425
  550.5 96.8 %collective-permute-start.71 = (bf16[2160,128]{1,0:T(8,128)(2,1)}, bf16[2160,128]{1,0:T(8,128)(2,1)}, u32[]{:S(2)}, u32[]{:S(2)}) collective-permute-start(bf16[2160,128]{1,0:T(8,128)(2,1)} %get-tuple-element.190), channel_id=1, source_target_pairs={{0,22},{2,20},{4,18},{6,16},{8,30},{10,28},{12,26},{14,24},{16,6},... | collective-permute-start | bytes 1658888 | tf_op jit(solution)/shard_map/ppermute | solution.py:425
  562.1 85.3 %collective-permute-start.72 = (bf16[2160,128]{1,0:T(8,128)(2,1)}, bf16[2160,128]{1,0:T(8,128)(2,1)}, u32[]{:S(2)}, u32[]{:S(2)}) collective-permute-start(bf16[2160,128]{1,0:T(8,128)(2,1)} %get-tuple-element.191), channel_id=1, source_target_pairs={{0,24},{2,26},{4,28},{6,30},{8,16},{10,18},{12,20},{14,22},{16,8},... | collective-permute-start | bytes 1658888 | tf_op jit(solution)/shard_map/ppermute | solution.py:425
  562.7 85.6 %collective-permute-start.73 = (bf16[2160,128]{1,0:T(8,128)(2,1)}, bf16[2160,128]{1,0:T(8,128)(2,1)}, u32[]{:S(2)}, u32[]{:S(2)}) collective-permute-start(bf16[2160,128]{1,0:T(8,128)(2,1)} %get-tuple-element.192), channel_id=1, source_target_pairs={{0,26},{2,24},{4,30},{6,28},{8,18},{10,16},{12,22},{14,20},{16,10}... | collective-permute-start | bytes 1658888 | tf_op jit(solution)/shard_map/ppermute | solution.py:425
  565.5 83.6 %collective-permute-start.74 = (bf16[2160,128]{1,0:T(8,128)(2,1)}, bf16[2160,128]{1,0:T(8,128)(2,1)}, u32[]{:S(2)}, u32[]{:S(2)}) collective-permute-start(bf16[2160,128]{1,0:T(8,128)(2,1)} %get-tuple-element.193), channel_id=1, source_target_pairs={{0,28},{2,30},{4,24},{6,26},{8,20},{10,22},{12,16},{14,18},{16,12}... | collective-permute-start | bytes 1658888 | tf_op jit(solution)/shard_map/ppermute | solution.py:425
  623.6 60.0 %collective-permute-start.75 = (bf16[2160,128]{1,0:T(8,128)(2,1)}, bf16[2160,128]{1,0:T(8,128)(2,1)}, u32[]{:S(2)}, u32[]{:S(2)}) collective-permute-start(bf16[2160,128]{1,0:T(8,128)(2,1)} %get-tuple-element.194), channel_id=1, source_target_pairs={{0,30},{2,28},{4,26},{6,24},{8,22},{10,20},{12,18},{14,16},{16,14}... | collective-permute-start | bytes 1658888 | tf_op jit(solution)/shard_map/ppermute | solution.py:425
  (120 other events, 5878.4 us)

commit v2 on v1

--- a/solution.py
+++ b/solution.py
@@ -165,6 +165,7 @@
 
 
 LANES = 128
+UNROLL = 3
 
 
 def fits(mesh, arrays):
@@ -176,11 +177,12 @@
     return all(c % 32 == 0 and (4 * c) % LANES == 0 for c in counts)
 
 
-def pack_kernel(counts, span, extra_mode, me_ref, *refs):
+def pack_kernel(counts, span, first, extra_mode, waits, me_ref, *refs):
     ins = refs[: len(counts)]
     refs = refs[len(counts) :]
     if extra_mode:
         extra, refs = refs[0], refs[1:]
+    refs = refs[waits:]
     outs, (buf, sems, extra_sems) = refs[:-3], refs[-3:]
     step = pl.program_id(0)
     steps = len(outs) // 2
@@ -221,7 +223,6 @@
         ).astype(jnp.bfloat16)
         base += count * span // LANES
 
-    first = me_ref[1]
     for index in range(steps):
 
         @pl.when(step == index)
@@ -258,25 +259,26 @@
                     ).wait()
 
 
-def pack(tensors, me, shards, first, steps, extra=None):
+def pack(tensors, me, shards, first, steps, extra=None, wait=()):
     span = tensors[0].shape[1] // shards
     counts = [t.shape[0] for t in tensors]
     bulk = sum(c * span // LANES for c in counts)
     mode = 0 if extra is None else extra.ndim - 1
     rows = bulk + (0 if extra is None else extra.shape[-2])
-    spot = jnp.stack([me, jnp.int32(first)])
-
-    def block(step, spot):
-        return (0, (spot[0] // 2) ^ (spot[1] + step))
+
+    def block(step, me):
+        return (0, (me[0] // 2) ^ (first + step))
 
     in_specs = [pl.BlockSpec((c, 2 * span), block) for c in counts]
     operands = list(tensors)
     if mode:
         in_specs.append(pl.BlockSpec(memory_space=pltpu.VMEM))
         operands.append(extra)
+    in_specs += [pl.BlockSpec(memory_space=pl.ANY)] * len(wait)
+    operands += list(wait)
     moved = sum(t.size for t in tensors) * 2 * steps // (shards // 2)
     return pl.pallas_call(
-        functools.partial(pack_kernel, counts, span, mode),
+        functools.partial(pack_kernel, counts, span, first, mode, len(wait)),
         grid_spec=pltpu.PrefetchScalarGridSpec(
             num_scalar_prefetch=1,
             grid=(steps,),
@@ -294,61 +296,53 @@
             flops=moved * 200, bytes_accessed=2 * moved, transcendentals=0
         ),
         name="pack",
-    )(spot, *operands)
+    )(me.reshape(1), *operands)
 
 
 def unpack_kernel(count, span, start, shards, me_ref, factor_ref, *refs):
     chunks = refs[:shards]
-    out, whole, shared, sems = refs[shards:]
+    out, landed, whole, shared, sems = refs[shards:]
     group = pl.program_id(0)
     me = me_ref[0]
     side = lax.rem(me, 2)
     lead = span // LANES
     half = count // 2
-
-    def copies(chunk, source):
-        at = pl.multiple_of(source * count, 32)
-        made = [
-            pltpu.make_async_copy(
-                chunk.at[pl.ds(start + tile * count, count)],
-                whole.at[tile, pl.ds(at, count)],
-                sems.at[source, tile],
-            )
-            for tile in range(lead)
-        ]
-        for part in range(2):
-            made.append(
-                pltpu.make_async_copy(
-                    chunk.at[pl.ds(start + lead * count, half)],
-                    shared.at[pl.ds(at + part * half, half)],
-                    sems.at[source, lead + part],
-                )
-            )
-        return made
+    height = count * span // LANES
+
+    def copy(chunk, source):
+        return pltpu.make_async_copy(
+            chunk.at[pl.ds(start, height)], landed.at[source], sems.at[source]
+        )
 
     @pl.when(group == 0)
     def _():
         for number in range(shards):
-            for copy in copies(chunks[number], me ^ number):
-                copy.start()
+            copy(chunks[number], me ^ number).start()
 
     for member in range(4):
-        for copy in copies(chunks[0], group * 4 + member):
-            copy.wait()
+        source = group * 4 + member
+        copy(chunks[0], source).wait()
+        for number in range(lead):
+            whole[number, pl.ds(member * count, count)] = landed[
+                source, pl.ds(number * count, count)
+            ]
+        tail = landed[source, pl.ds(lead * count, half)]
+        shared[pl.ds(member * count, half)] = tail
+        shared[pl.ds(member * count + half, half)] = tail
 
     factor = factor_ref[0]
     rise = pl.multiple_of(side * (LANES // 2), LANES // 2)
     fall = pl.multiple_of((1 - side) * (lead * LANES), LANES // 2)
 
     def tile_step(tile, carry):
-        row = pl.multiple_of(group * (4 * count) + tile * LANES, LANES)
-        column = pl.ds(pl.multiple_of(tile * LANES, LANES), LANES)
+        row = pl.multiple_of(tile * LANES, LANES)
+        column = pl.ds(row, LANES)
         for number in range(lead):
-            piece = whole[number, pl.ds(row, LANES), :].astype(jnp.float32)
+            piece = whole[number, pl.ds(row, LANES), :].T.astype(jnp.float32)
             out[pl.ds(pl.multiple_of(rise + number * LANES, LANES // 2), LANES), column] = (
-                piece.T * factor
+                piece * factor
             ).astype(jnp.bfloat16)
-        piece = shared[pl.ds(row, LANES), :].astype(jnp.float32).T
+        piece = shared[pl.ds(row, LANES), :].T.astype(jnp.float32)
         spot = row + lax.broadcasted_iota(jnp.int32, (LANES // 2, LANES), 1)
         low = lax.rem(spot, count) < half
         out[pl.ds(fall, LANES // 2), column] = (
@@ -356,7 +350,7 @@
         ).astype(jnp.bfloat16)
         return carry
 
-    lax.fori_loop(0, 4 * count // LANES, tile_step, 0)
+    lax.fori_loop(0, 4 * count // LANES, tile_step, 0, unroll=UNROLL)
 
 
 def unpack(chunks, me, factor, count, span, start):
@@ -370,9 +364,10 @@
             in_specs=[pl.BlockSpec(memory_space=pl.ANY)] * shards,
             out_specs=pl.BlockSpec((span, 4 * count), lambda group, me, factor: (0, group)),
             scratch_shapes=[
-                pltpu.VMEM((span // LANES, shards * count, LANES), jnp.bfloat16),
-                pltpu.VMEM((shards * count, LANES), jnp.bfloat16),
-                pltpu.SemaphoreType.DMA((shards, span // LANES + 2)),
+                pltpu.VMEM((shards, count * span // LANES, LANES), jnp.bfloat16),
+                pltpu.VMEM((span // LANES, 4 * count, LANES), jnp.bfloat16),
+                pltpu.VMEM((4 * count, LANES), jnp.bfloat16),
+                pltpu.SemaphoreType.DMA((shards,)),
             ],
         ),
         out_shape=jax.ShapeDtypeStruct((span, shards * count), jnp.bfloat16),
@@ -384,28 +379,28 @@
     )(me.reshape(1), factor.reshape(1), *chunks)
 
 
-def collect_kernel(start, height, me_ref, *refs):
+def collect_kernel(places, height, me_ref, *refs):
     chunks, out, sems = refs[:-2], refs[-2], refs[-1]
-
-    def copy(number):
-        return pltpu.make_async_copy(
-            chunks[number].at[pl.ds(start, height)], out.at[me_ref[0] ^ number], sems.at[number]
+    copies = [
+        pltpu.make_async_copy(
+            chunks[chunk].at[pl.ds(start, height)], out.at[me_ref[0] ^ number], sems.at[number]
         )
-
-    for number in range(len(chunks)):
-        copy(number).start()
-    for number in range(len(chunks)):
-        copy(number).wait()
-
-
-def collect(chunks, me, start, height):
-    shards = len(chunks)
+        for number, (chunk, start) in enumerate(places)
+    ]
+    for copy in copies:
+        copy.start()
+    for copy in copies:
+        copy.wait()
+
+
+def collect(chunks, me, places, height):
+    shards = len(places)
     return pl.pallas_call(
-        functools.partial(collect_kernel, start, height),
+        functools.partial(collect_kernel, places, height),
         grid_spec=pltpu.PrefetchScalarGridSpec(
             num_scalar_prefetch=1,
             grid=(1,),
-            in_specs=[pl.BlockSpec(memory_space=pl.ANY)] * shards,
+            in_specs=[pl.BlockSpec(memory_space=pl.ANY)] * len(chunks),
             out_specs=pl.BlockSpec((shards, height, LANES), lambda step, me: (0, 0, 0)),
             scratch_shapes=[pltpu.SemaphoreType.DMA((shards,))],
         ),
@@ -418,7 +413,7 @@
 
 
 def exchange(chunks, order):
-    shards = len(chunks)
+    shards = lax.axis_size("fsdp")
     arrived = list(chunks)
     for number in order:
         pairs = [(source, source ^ number) for source in range(shards)]
@@ -463,44 +458,58 @@
     query_t, key_t, value_t = query_weight.T, key_weight.T, value_weight.T
     gate_t, up_t = gate_weight.T, up_weight.T
     cross = shards // 2
+    pairs = shards // 2
     mixed = [cross]
     for number in range(1, cross):
         mixed += [number, cross + number]
-    pairs = shards // 2
 
     def rows(tensor):
         return tensor.shape[0] * span // LANES
 
-    wire_hidden = hidden.reshape(seqs * span // LANES, LANES)
-    far = pack([gate_t], me, shards, pairs // 2, pairs // 2, wire_hidden)
-    gate_near, hidden_near = after(far[0], gate_t, wire_hidden)
-    near = pack([gate_near], me, shards, 0, pairs // 2, hidden_near)
-    gate_chunks = near + far
-    gate_chunks = exchange(gate_chunks, list(range(cross, shards)))
-    gate_chunks = exchange(gate_chunks, list(range(1, cross)))
+    far, near = range(cross, shards), range(1, cross)
+    lower, fourth = pairs // 2, pairs // 4
+    height = seqs * span // LANES
+    gate_far = pack([gate_t], me, shards, lower, fourth)
+    (hidden_late,) = after(gate_far[0], hidden)
+    own_hidden = hidden_late.reshape(height, LANES)
+    other_hidden = exchange([own_hidden] * shards, [cross])[cross]
 
     trainer = (query_t, key_t, value_t, output_weight, gate_t, up_t, down_weight)
-    staged = after(near[0], *trainer)
+    staged = after(gate_far[0], *trainer)
     local = jnp.stack([largest(tensor) for tensor in staged])
     tile = jnp.broadcast_to(jnp.pad(local, (0, 9))[:, None], (16, LANES)).astype(jnp.bfloat16)
     best = tile
     for turn in range(1, half):
         ring = [(source, (source + turn) % half) for source in range(half)]
         best = jnp.maximum(best, lax.ppermute(tile, "tp", ring))
-    up_chunks = pack([up_t], me, shards, 0, pairs, best)
-    (down_late,) = after(up_chunks[0], down_weight)
-    down_chunks = pack([down_late], me, shards, 0, pairs)
-    up_chunks = exchange(up_chunks, mixed)
-    down_chunks = exchange(down_chunks, mixed)
-
-    everyone = collect(gate_chunks, me, rows(gate_t), wire_hidden.shape[0])
+    low = best.shape[0]
+    pair_far = pack([key_t, value_t], me, shards, lower, lower, best)
+    key_late, value_late = after(pair_far[0], key_t, value_t)
+    both = jnp.concatenate([best, own_hidden, other_hidden], axis=0)
+    pair_near = pack([key_late, value_late], me, shards, 0, lower, both)
+    pair_chunks = pair_near + pair_far
+    pair_chunks = exchange(pair_chunks, far)
+    pair_chunks = exchange(pair_chunks, near)
+    (gate_two,) = after(pair_near[0], gate_t)
+    gate_far += pack([gate_two], me, shards, lower + fourth, lower - fourth)
+    (gate_two,) = after(gate_far[-1], gate_t)
+    gate_near = pack([gate_two], me, shards, 0, lower)
+    gate_chunks = gate_near + gate_far
+    split = cross + 2 * fourth
+    gate_chunks = exchange(gate_chunks, range(cross, cross + 1))
+    gate_chunks = exchange(gate_chunks, range(cross + 1, split))
+    gate_chunks = exchange(gate_chunks, range(split, shards))
+    gate_chunks = exchange(gate_chunks, near)
+
+    bulk = rows(key_t) + rows(value_t)
+    seen = collect(pair_chunks, me, [(number, bulk) for number in range(shards)], low)
+    peaks = jnp.max(seen[:, :7, 0].astype(jnp.float32), axis=0)
+    factors, new_history = scaling(peaks, history, slot)
+    places = [(number % cross, bulk + low + number // cross * height) for number in range(shards)]
+    everyone = collect(pair_chunks[:cross], me, places, height)
     everyone = everyone.reshape(shards, seqs, span).transpose(1, 0, 2).reshape(seqs, shards * span)
     widened = everyone.astype(jnp.float32)
     inv_rms = lax.rsqrt(jnp.sum(widened * widened, axis=1) / D + norm_eps)[:, None]
-
-    seen = collect(up_chunks, me, rows(up_t), best.shape[0])
-    peaks = jnp.max(seen[:, :7, 0].astype(jnp.float32), axis=0)
-    factors, new_history = scaling(peaks, history, slot)
 
     parts = []
     for number, tensor in enumerate((query_t, key_t, value_t)):
@@ -520,13 +529,15 @@
     used = terms.shape[1]
     filled = -(-used // 16) * 16
     terms = jnp.pad(terms, ((0, 0), (0, filled - used), (0, 0)))
-    output_chunks = pack([output_weight], me, shards, 0, pairs, terms)
-    query_late, key_late, value_late = after(output_chunks[0], query_t, key_t, value_t)
-    last = pack([query_late, key_late, value_late], me, shards, 0, pairs)
+    up_chunks = pack([up_t, query_t], me, shards, 0, pairs, terms)
+    up_chunks = exchange(up_chunks, mixed)
+    down_chunks = pack([down_weight], me, shards, 0, pairs, None, gate_chunks[1:])
+    down_chunks = exchange(down_chunks, mixed)
+    places = [(number, rows(up_t) + rows(query_t)) for number in range(shards)]
+    mine = collect(up_chunks, me, places, filled)
+    output_chunks = pack([output_weight], me, shards, 0, pairs, None, (mine,))
     output_chunks = exchange(output_chunks, mixed)
-    last = exchange(last, mixed)
-
-    mine = collect(output_chunks, me, rows(output_weight), filled)[:, :used]
+    mine = mine[:, :used]
     mine = mine.reshape(shards, share, 3, padded).astype(jnp.float32)
     mine = (mine[:, :, 2] + mine[:, :, 1] + mine[:, :, 0]).transpose(1, 0, 2)
     width_q, width_k = query_t.shape[0], key_t.shape[0]
@@ -544,9 +555,9 @@
 
     return (
         attention_out,
-        finish(last, 0, query_t),
-        finish(last, 1, key_t, rows(query_t)),
-        finish(last, 2, value_t, rows(query_t) + rows(key_t)),
+        finish(up_chunks, 0, query_t, rows(up_t)),
+        finish(pair_chunks, 1, key_t),
+        finish(pair_chunks, 2, value_t, rows(key_t)),
         finish(output_chunks, 3, output_weight).T,
         finish(gate_chunks, 4, gate_t),
         finish(up_chunks, 5, up_t),

time: 861 us -> 825 us (0.958)
  the two profiles are of different devices: /device:TPU:0 before, /device:TPU:17 now
where the time goes in v2:
time: 825 us; the launch traced here: 823 us
  waiting for transfers between devices  552 us (67%)
  starting transfers between devices  115 us (14%)
  Pallas kernels  97.3 us (12%)
  other arithmetic  24.7 us (3%)
  local copies, waits for them, and re-layouts  16.7 us (2%)
  matrix products  14.5 us (2%)
    ppermute x76, waiting for transfers between devices, exchange(): arrived[number] = lax.ppermute(chunks[number], 'fsdp', pairs)  552 us
    ppermute x76, starting transfers between devices, exchange(): arrived[number] = lax.ppermute(chunks[number], 'fsdp', pairs)  114 us
    pallas_call x7, Pallas kernels, unpack(): pl.pallas_call(functools.partial(unpack_kernel, count, span, start, shard...  49.4 us
    pallas_call x8, Pallas kernels, pack(): pl.pallas_call(functools.partial(pack_kernel, counts, span, first, mode,...  43 us
    reduce_max x4, other arithmetic, largest(): return jnp.max(jnp.abs(tensor.astype(jnp.float32)))  18 us
  transfers between devices with their start and end apart: 77, of which 41 were waited for; matrix products, arithmetic and copies ran while one was open for 3% of the time, Pallas kernels for 9%

profile of v2, /device:TPU:17, one launch (start us, length us, event | category | flops | bytes accessed | tf_op | source)
XLA Modules:
  0.0 823.3 jit_solution(6769600658346039520)
XLA Ops:
  11.2 10.6 %abs_reduce_fusion = (bf16[]{:T(256)}, bf16[]{:T(256)}) fusion(bf16[864,5120]{1,0:T(8,128)(2,1)} %refs_0_.3, bf16[864,5120]{1,0:T(8,128)(2,1)} %bitcast.79), kind=kLoop, calls=%fused_computation | loop fusion | flops 26542080 | bytes 17694724 | tf_op jit(solution)/shard_map/reduce_max | solution.py:23
  81.0 52.1 %collective-permute-done.54.refs_8_ = bf16[2160,128]{1,0:T(8,128)(2,1)S(1)} collective-permute-done((bf16[2160,128]{1,0:T(8,128)(2,1)}, bf16[2160,128]{1,0:T(8,128)(2,1)S(1)}, u32[]{:S(2)}, u32[]{:S(2)}) %collective-permute-start.54) | collective-permute-done | bytes 552992 | tf_op jit(solution)/shard_map/ppermute | solution.py:420
  134.0 11.0 %collective-permute-done.55.refs_9_ = bf16[2160,128]{1,0:T(8,128)(2,1)} collective-permute-done((bf16[2160,128]{1,0:T(8,128)(2,1)}, bf16[2160,128]{1,0:T(8,128)(2,1)}, u32[]{:S(2)}, u32[]{:S(2)}) %collective-permute-start.55) | collective-permute-done | bytes 552992 | tf_op jit(solution)/shard_map/ppermute | solution.py:420
  146.1 10.7 %collective-permute-done.56.refs_10_ = bf16[2160,128]{1,0:T(8,128)(2,1)} collective-permute-done((bf16[2160,128]{1,0:T(8,128)(2,1)}, bf16[2160,128]{1,0:T(8,128)(2,1)}, u32[]{:S(2)}, u32[]{:S(2)}) %collective-permute-start.56) | collective-permute-done | bytes 552992 | tf_op jit(solution)/shard_map/ppermute | solution.py:420
  160.0 8.8 %collective-permute-done.57.refs_11_ = bf16[2160,128]{1,0:T(8,128)(2,1)} collective-permute-done((bf16[2160,128]{1,0:T(8,128)(2,1)}, bf16[2160,128]{1,0:T(8,128)(2,1)}, u32[]{:S(2)}, u32[]{:S(2)}) %collective-permute-start.57) | collective-permute-done | bytes 552992 | tf_op jit(solution)/shard_map/ppermute | solution.py:420
  179.3 6.6 collective-permute-start.53
  193.9 11.2 %collective-permute-done.52.refs_6_ = bf16[2160,128]{1,0:T(8,128)(2,1)} collective-permute-done((bf16[2160,128]{1,0:T(8,128)(2,1)}, bf16[2160,128]{1,0:T(8,128)(2,1)}, u32[]{:S(2)}, u32[]{:S(2)}) %collective-permute-start.52) | collective-permute-done | bytes 552992 | tf_op jit(solution)/shard_map/ppermute | solution.py:420
  208.9 10.9 %pack.11 = (bf16[2576,128]{1,0:T(8,128)(2,1)}, bf16[2576,128]{1,0:T(8,128)(2,1)}, bf16[2576,128]{1,0:T(8,128)(2,1)}, bf16[2576,128]{1,0:T(8,128)(2,1)}, bf16[257...) custom-call(s32[1]{0:T(128)} %bitcast.me_ref, ...), custom_call_target="tpu_custom_call" | custom-call | flops 2097152000 | bytes 20971520 | tf_op jit(solution)/shard_map/pack/pallas_call | solution.py:280
  219.7 9.9 %collective-permute-done.53.refs_7_ = bf16[2160,128]{1,0:T(8,128)(2,1)S(1)} collective-permute-done((bf16[2160,128]{1,0:T(8,128)(2,1)}, bf16[2160,128]{1,0:T(8,128)(2,1)S(1)}, u32[]{:S(2)}, u32[]{:S(2)}) %collective-permute-start.53) | collective-permute-done | bytes 552992 | tf_op jit(solution)/shard_map/ppermute | solution.py:420
  231.7 39.9 %collective-permute-done.59.refs_13_ = bf16[2160,128]{1,0:T(8,128)(2,1)} collective-permute-done((bf16[2160,128]{1,0:T(8,128)(2,1)}, bf16[2160,128]{1,0:T(8,128)(2,1)}, u32[]{:S(2)}, u32[]{:S(2)}) %collective-permute-start.59) | collective-permute-done | bytes 552992 | tf_op jit(solution)/shard_map/ppermute | solution.py:420
  272.7 11.2 %collective-permute-done.60.refs_14_ = bf16[2160,128]{1,0:T(8,128)(2,1)} collective-permute-done((bf16[2160,128]{1,0:T(8,128)(2,1)}, bf16[2160,128]{1,0:T(8,128)(2,1)}, u32[]{:S(2)}, u32[]{:S(2)}) %collective-permute-start.60) | collective-permute-done | bytes 552992 | tf_op jit(solution)/shard_map/ppermute | solution.py:420
  289.1 8.8 %collective-permute-done.19.refs_3_ = bf16[2576,128]{1,0:T(8,128)(2,1)S(1)} collective-permute-done((bf16[2576,128]{1,0:T(8,128)(2,1)}, bf16[2576,128]{1,0:T(8,128)(2,1)S(1)}, u32[]{:S(2)}, u32[]{:S(2)}) %collective-permute-start.19) | collective-permute-done | bytes 659488 | tf_op jit(solution)/shard_map/ppermute | solution.py:420
  302.3 38.3 %collective-permute-done.21.refs_5_ = bf16[2576,128]{1,0:T(8,128)(2,1)S(1)} collective-permute-done((bf16[2576,128]{1,0:T(8,128)(2,1)}, bf16[2576,128]{1,0:T(8,128)(2,1)S(1)}, u32[]{:S(2)}, u32[]{:S(2)}) %collective-permute-start.21) | collective-permute-done | bytes 659488 | tf_op jit(solution)/shard_map/ppermute | solution.py:420
  344.6 10.3 %collective-permute-done.22.refs_6_ = bf16[2576,128]{1,0:T(8,128)(2,1)} collective-permute-done((bf16[2576,128]{1,0:T(8,128)(2,1)}, bf16[2576,128]{1,0:T(8,128)(2,1)}, u32[]{:S(2)}, u32[]{:S(2)}) %collective-permute-start.22) | collective-permute-done | bytes 659488 | tf_op jit(solution)/shard_map/ppermute | solution.py:420
  360.0 9.1 %collective-permute-done.23.refs_7_ = bf16[2576,128]{1,0:T(8,128)(2,1)} collective-permute-done((bf16[2576,128]{1,0:T(8,128)(2,1)}, bf16[2576,128]{1,0:T(8,128)(2,1)}, u32[]{:S(2)}, u32[]{:S(2)}) %collective-permute-start.23) | collective-permute-done | bytes 659488 | tf_op jit(solution)/shard_map/ppermute | solution.py:420
  374.0 81.5 %collective-permute-done.26.refs_10_ = bf16[2576,128]{1,0:T(8,128)(2,1)} collective-permute-done((bf16[2576,128]{1,0:T(8,128)(2,1)}, bf16[2576,128]{1,0:T(8,128)(2,1)}, u32[]{:S(2)}, u32[]{:S(2)}) %collective-permute-start.26) | collective-permute-done | bytes 659488 | tf_op jit(solution)/shard_map/ppermute | solution.py:420
  463.7 11.2 %unpack.11 = bf16[320,13824]{1,0:T(8,128)(2,1)} custom-call(s32[1]{0:T(128)} %bitcast.me_ref, f32[1]{0:T(128)} %get-tuple-element.211.factor_ref, bf16[2160,128]{1,0:T(8,128)(2,1)} %get-tuple-element.163.refs_0_, bf16[2160,128]{1,0:T(8,128)(2,1)} %collective-permute-done.47.refs_1_, bf16[2160,128]{1,0:T(8,128)(2,1)} %collective-permute-done.48.refs_2_, ...), custom_call_target="tpu_custom_call" | custom-call | flops 884736000 | bytes 17694720 | tf_op jit(solution)/shard_map/unpack/pallas_call | solution.py:359
  474.9 9.9 %pack.15 = (bf16[2160,128]{1,0:T(8,128)(2,1)}, bf16[2160,128]{1,0:T(8,128)(2,1)}, bf16[2160,128]{1,0:T(8,128)(2,1)}, bf16[2160,128]{1,0:T(8,128)(2,1)}, bf16[216...) custom-call(s32[1]{0:T(128)} %bitcast.me_ref, ...), custom_call_target="tpu_custom_call" | custom-call | flops 1769472000 | bytes 17694720 | tf_op jit(solution)/shard_map/pack/pallas_call | solution.py:280
  484.9 14.4 %collective-permute-done.28.refs_12_ = bf16[2576,128]{1,0:T(8,128)(2,1)} collective-permute-done((bf16[2576,128]{1,0:T(8,128)(2,1)}, bf16[2576,128]{1,0:T(8,128)(2,1)}, u32[]{:S(2)}, u32[]{:S(2)}) %collective-permute-start.28) | collective-permute-done | bytes 659488 | tf_op jit(solution)/shard_map/ppermute | solution.py:420
  499.3 14.1 %collective-permute-done.29.refs_13_ = bf16[2576,128]{1,0:T(8,128)(2,1)} collective-permute-done((bf16[2576,128]{1,0:T(8,128)(2,1)}, bf16[2576,128]{1,0:T(8,128)(2,1)}, u32[]{:S(2)}, u32[]{:S(2)}) %collective-permute-start.29) | collective-permute-done | bytes 659488 | tf_op jit(solution)/shard_map/ppermute | solution.py:420
  513.5 14.6 %collective-permute-done.30.refs_14_ = bf16[2576,128]{1,0:T(8,128)(2,1)} collective-permute-done((bf16[2576,128]{1,0:T(8,128)(2,1)}, bf16[2576,128]{1,0:T(8,128)(2,1)}, u32[]{:S(2)}, u32[]{:S(2)}) %collective-permute-start.30) | collective-permute-done | bytes 659488 | tf_op jit(solution)/shard_map/ppermute | solution.py:420
  528.1 14.1 %collective-permute-done.31.refs_15_ = bf16[2576,128]{1,0:T(8,128)(2,1)} collective-permute-done((bf16[2576,128]{1,0:T(8,128)(2,1)}, bf16[2576,128]{1,0:T(8,128)(2,1)}, u32[]{:S(2)}, u32[]{:S(2)}) %collective-permute-start.31) | collective-permute-done | bytes 659488 | tf_op jit(solution)/shard_map/ppermute | solution.py:420
  570.7 8.4 %collective-permute-done.41.refs_10_ = bf16[400,128]{1,0:T(8,128)(2,1)S(1)} collective-permute-done((bf16[400,128]{1,0:T(8,128)(2,1)}, bf16[400,128]{1,0:T(8,128)(2,1)S(1)}, u32[]{:S(2)}, u32[]{:S(2)}) %collective-permute-start.41) | collective-permute-done | bytes 102432 | tf_op jit(solution)/shard_map/ppermute | solution.py:420
  608.2 11.8 %collective-permute-done.64.refs_3_ = bf16[2160,128]{1,0:T(8,128)(2,1)S(1)} collective-permute-done((bf16[2160,128]{1,0:T(8,128)(2,1)}, bf16[2160,128]{1,0:T(8,128)(2,1)S(1)}, u32[]{:S(2)}, u32[]{:S(2)}) %collective-permute-start.64) | collective-permute-done | bytes 552992 | tf_op jit(solution)/shard_map/ppermute | solution.py:420
  623.8 29.4 %collective-permute-done.67.refs_6_ = bf16[2160,128]{1,0:T(8,128)(2,1)S(1)} collective-permute-done((bf16[2160,128]{1,0:T(8,128)(2,1)S(1)}, bf16[2160,128]{1,0:T(8,128)(2,1)S(1)}, u32[]{:S(2)}, u32[]{:S(2)}) %collective-permute-start.67) | collective-permute-done | bytes 552992 | tf_op jit(solution)/shard_map/ppermute | solution.py:420
  671.6 66.9 %collective-permute-done.71.refs_10_ = bf16[2160,128]{1,0:T(8,128)(2,1)} collective-permute-done((bf16[2160,128]{1,0:T(8,128)(2,1)S(1)}, bf16[2160,128]{1,0:T(8,128)(2,1)}, u32[]{:S(2)}, u32[]{:S(2)}) %collective-permute-start.71) | collective-permute-done | bytes 552992 | tf_op jit(solution)/shard_map/ppermute | solution.py:420
  751.3 11.1 %unpack.12 = bf16[320,13824]{1,0:T(8,128)(2,1)} custom-call(s32[1]{0:T(128)} %bitcast.me_ref, f32[1]{0:T(128)} %get-tuple-element.210.factor_ref, bf16[2576,128]{1,0:T(8,128)(2,1)} %get-tuple-element.128.refs_0_, bf16[2576,128]{1,0:T(8,128)(2,1)} %copy-done.2, bf16[2576,128]{1,0:T(8,128)(2,1)} %copy-done.3, bf16[2576,128]{1,0:T(8,128)(2,1)} %copy-done.4, ...), custom_call_target="tpu_custom_call" | custom-call | flops 884736000 | bytes 17694720 | tf_op jit(solution)/shard_map/unpack/pallas_call | solution.py:359
  767.3 8.4 %collective-permute-done.73.refs_12_ = bf16[2160,128]{1,0:T(8,128)(2,1)} collective-permute-done((bf16[2160,128]{1,0:T(8,128)(2,1)}, bf16[2160,128]{1,0:T(8,128)(2,1)}, u32[]{:S(2)}, u32[]{:S(2)}) %collective-permute-start.73) | collective-permute-done | bytes 552992 | tf_op jit(solution)/shard_map/ppermute | solution.py:420
  775.6 12.7 %collective-permute-done.74.refs_13_ = bf16[2160,128]{1,0:T(8,128)(2,1)} collective-permute-done((bf16[2160,128]{1,0:T(8,128)(2,1)}, bf16[2160,128]{1,0:T(8,128)(2,1)}, u32[]{:S(2)}, u32[]{:S(2)}) %collective-permute-start.74) | collective-permute-done | bytes 552992 | tf_op jit(solution)/shard_map/ppermute | solution.py:420
  788.3 11.5 %collective-permute-done.75.refs_14_ = bf16[2160,128]{1,0:T(8,128)(2,1)} collective-permute-done((bf16[2160,128]{1,0:T(8,128)(2,1)}, bf16[2160,128]{1,0:T(8,128)(2,1)}, u32[]{:S(2)}, u32[]{:S(2)}) %collective-permute-start.75) | collective-permute-done | bytes 552992 | tf_op jit(solution)/shard_map/ppermute | solution.py:420
  799.8 12.1 %collective-permute-done.76.refs_15_ = bf16[2160,128]{1,0:T(8,128)(2,1)} collective-permute-done((bf16[2160,128]{1,0:T(8,128)(2,1)}, bf16[2160,128]{1,0:T(8,128)(2,1)}, u32[]{:S(2)}, u32[]{:S(2)}) %collective-permute-start.76) | collective-permute-done | bytes 552992 | tf_op jit(solution)/shard_map/ppermute | solution.py:420
  812.0 11.1 %unpack.13 = bf16[320,13824]{1,0:T(8,128)(2,1)} custom-call(s32[1]{0:T(128)} %bitcast.me_ref, f32[1]{0:T(128)} %get-tuple-element.209.factor_ref, bf16[2160,128]{1,0:T(8,128)(2,1)} %get-tuple-element.177.refs_0_, bf16[2160,128]{1,0:T(8,128)(2,1)} %copy-done.22, bf16[2160,128]{1,0:T(8,128)(2,1)} %copy-done.23, bf16[2160,128]{1,0:T(8,128)(2,1)} %copy-done.24, ...), custom_call_target="tpu_custom_call" | custom-call | flops 884736000 | bytes 17694720 | tf_op jit(solution)/shard_map/unpack/pallas_call | solution.py:359
  (322 shorter events, 228.3 us)
Async XLA Ops:
  68.8 64.3 %collective-permute-start.54 = (bf16[2160,128]{1,0:T(8,128)(2,1)}, bf16[2160,128]{1,0:T(8,128)(2,1)S(1)}, u32[]{:S(2)}, u32[]{:S(2)}) collective-permute-start(bf16[2160,128]{1,0:T(8,128)(2,1)} %get-tuple-element.101), channel_id=1, source_target_pairs={{0,16},{2,18},{4,20},{6,22},{8,24},{10,26},{12,28},{14,30},{16,0},... | collective-permute-start | bytes 1658888 | tf_op jit(solution)/shard_map/ppermute | solution.py:420
  73.8 71.2 %collective-permute-start.55 = (bf16[2160,128]{1,0:T(8,128)(2,1)}, bf16[2160,128]{1,0:T(8,128)(2,1)}, u32[]{:S(2)}, u32[]{:S(2)}) collective-permute-start(bf16[2160,128]{1,0:T(8,128)(2,1)} %get-tuple-element.171), channel_id=1, source_target_pairs={{0,18},{2,16},{4,22},{6,20},{8,26},{10,24},{12,30},{14,28},{16,2},... | collective-permute-start | bytes 1658888 | tf_op jit(solution)/shard_map/ppermute | solution.py:420
  73.8 83.0 %collective-permute-start.56 = (bf16[2160,128]{1,0:T(8,128)(2,1)}, bf16[2160,128]{1,0:T(8,128)(2,1)}, u32[]{:S(2)}, u32[]{:S(2)}) collective-permute-start(bf16[2160,128]{1,0:T(8,128)(2,1)} %get-tuple-element.172), channel_id=1, source_target_pairs={{0,20},{2,22},{4,16},{6,18},{8,28},{10,30},{12,24},{14,26},{16,4},... | collective-permute-start | bytes 1658888 | tf_op jit(solution)/shard_map/ppermute | solution.py:420
  75.7 93.0 %collective-permute-start.57 = (bf16[2160,128]{1,0:T(8,128)(2,1)}, bf16[2160,128]{1,0:T(8,128)(2,1)}, u32[]{:S(2)}, u32[]{:S(2)}) collective-permute-start(bf16[2160,128]{1,0:T(8,128)(2,1)} %get-tuple-element.173), channel_id=1, source_target_pairs={{0,22},{2,20},{4,18},{6,16},{8,30},{10,28},{12,26},{14,24},{16,6},... | collective-permute-start | bytes 1658888 | tf_op jit(solution)/shard_map/ppermute | solution.py:420
  77.7 94.5 %collective-permute-start.47 = (bf16[2160,128]{1,0:T(8,128)(2,1)}, bf16[2160,128]{1,0:T(8,128)(2,1)}, u32[]{:S(2)}, u32[]{:S(2)}) collective-permute-start(bf16[2160,128]{1,0:T(8,128)(2,1)} %get-tuple-element.164), channel_id=1, source_target_pairs={{0,2},{2,0},{4,6},{6,4},{8,10},{10,8},{12,14},{14,12},{16,18},{18,... | collective-permute-start | bytes 1658888 | tf_op jit(solution)/shard_map/ppermute | solution.py:420
  177.5 106.5 %collective-permute-start.61 = (bf16[2160,128]{1,0:T(8,128)(2,1)}, bf16[2160,128]{1,0:T(8,128)(2,1)S(1)}, u32[]{:S(2)}, u32[]{:S(2)}) collective-permute-start(bf16[2160,128]{1,0:T(8,128)(2,1)} %get-tuple-element.161), channel_id=1, source_target_pairs={{0,30},{2,28},{4,26},{6,24},{8,22},{10,20},{12,18},{14,16},{16,14}... | collective-permute-start | bytes 1658888 | tf_op jit(solution)/shard_map/ppermute | solution.py:420
  179.3 50.4 %collective-permute-start.53 = (bf16[2160,128]{1,0:T(8,128)(2,1)}, bf16[2160,128]{1,0:T(8,128)(2,1)S(1)}, u32[]{:S(2)}, u32[]{:S(2)}) collective-permute-start(bf16[2160,128]{1,0:T(8,128)(2,1)} %get-tuple-element.170), channel_id=1, source_target_pairs={{0,14},{2,12},{4,10},{6,8},{8,6},{10,4},{12,2},{14,0},{16,30},{18,... | collective-permute-start | bytes 1658888 | tf_op jit(solution)/shard_map/ppermute | solution.py:420
  193.0 78.6 %collective-permute-start.59 = (bf16[2160,128]{1,0:T(8,128)(2,1)}, bf16[2160,128]{1,0:T(8,128)(2,1)}, u32[]{:S(2)}, u32[]{:S(2)}) collective-permute-start(bf16[2160,128]{1,0:T(8,128)(2,1)} %get-tuple-element.175), channel_id=1, source_target_pairs={{0,26},{2,24},{4,30},{6,28},{8,18},{10,16},{12,22},{14,20},{16,10}... | collective-permute-start | bytes 1658888 | tf_op jit(solution)/shard_map/ppermute | solution.py:420
  205.1 78.8 %collective-permute-start.60 = (bf16[2160,128]{1,0:T(8,128)(2,1)}, bf16[2160,128]{1,0:T(8,128)(2,1)}, u32[]{:S(2)}, u32[]{:S(2)}) collective-permute-start(bf16[2160,128]{1,0:T(8,128)(2,1)} %get-tuple-element.176), channel_id=1, source_target_pairs={{0,28},{2,30},{4,24},{6,26},{8,20},{10,22},{12,16},{14,18},{16,12}... | collective-permute-start | bytes 1658888 | tf_op jit(solution)/shard_map/ppermute | solution.py:420
  230.5 56.3 %collective-permute-start.17 = (bf16[2576,128]{1,0:T(8,128)(2,1)}, bf16[2576,128]{1,0:T(8,128)(2,1)S(1)}, u32[]{:S(2)}, u32[]{:S(2)}) collective-permute-start(bf16[2576,128]{1,0:T(8,128)(2,1)} %get-tuple-element.129), channel_id=1, source_target_pairs={{0,2},{2,0},{4,6},{6,4},{8,10},{10,8},{12,14},{14,12},{16,18},{18,... | collective-permute-start | bytes 1978376 | tf_op jit(solution)/shard_map/ppermute | solution.py:420
  230.5 56.4 %collective-permute-start.18 = (bf16[2576,128]{1,0:T(8,128)(2,1)}, bf16[2576,128]{1,0:T(8,128)(2,1)S(1)}, u32[]{:S(2)}, u32[]{:S(2)}) collective-permute-start(bf16[2576,128]{1,0:T(8,128)(2,1)} %get-tuple-element.130), channel_id=1, source_target_pairs={{0,4},{2,6},{4,0},{6,2},{8,12},{10,14},{12,8},{14,10},{16,20},{18,... | collective-permute-start | bytes 1978376 | tf_op jit(solution)/shard_map/ppermute | solution.py:420
  284.7 55.9 %collective-permute-start.21 = (bf16[2576,128]{1,0:T(8,128)(2,1)}, bf16[2576,128]{1,0:T(8,128)(2,1)S(1)}, u32[]{:S(2)}, u32[]{:S(2)}) collective-permute-start(bf16[2576,128]{1,0:T(8,128)(2,1)} %get-tuple-element.133), channel_id=1, source_target_pairs={{0,10},{2,8},{4,14},{6,12},{8,2},{10,0},{12,6},{14,4},{16,26},{18,... | collective-permute-start | bytes 1978376 | tf_op jit(solution)/shard_map/ppermute | solution.py:420
  286.8 68.1 %collective-permute-start.22 = (bf16[2576,128]{1,0:T(8,128)(2,1)}, bf16[2576,128]{1,0:T(8,128)(2,1)}, u32[]{:S(2)}, u32[]{:S(2)}) collective-permute-start(bf16[2576,128]{1,0:T(8,128)(2,1)} %get-tuple-element.134), channel_id=1, source_target_pairs={{0,12},{2,14},{4,8},{6,10},{8,4},{10,6},{12,0},{14,2},{16,28},{18,... | collective-permute-start | bytes 1978376 | tf_op jit(solution)/shard_map/ppermute | solution.py:420
  287.0 82.1 %collective-permute-start.23 = (bf16[2576,128]{1,0:T(8,128)(2,1)}, bf16[2576,128]{1,0:T(8,128)(2,1)}, u32[]{:S(2)}, u32[]{:S(2)}) collective-permute-start(bf16[2576,128]{1,0:T(8,128)(2,1)} %get-tuple-element.135), channel_id=1, source_target_pairs={{0,14},{2,12},{4,10},{6,8},{8,6},{10,4},{12,2},{14,0},{16,30},{18,... | collective-permute-start | bytes 1978376 | tf_op jit(solution)/shard_map/ppermute | solution.py:420
  298.0 71.7 %collective-permute-start.24 = (bf16[2576,128]{1,0:T(8,128)(2,1)}, bf16[2576,128]{1,0:T(8,128)(2,1)}, u32[]{:S(2)}, u32[]{:S(2)}) collective-permute-start(bf16[2576,128]{1,0:T(8,128)(2,1)} %get-tuple-element.136), channel_id=1, source_target_pairs={{0,16},{2,18},{4,20},{6,22},{8,24},{10,26},{12,28},{14,30},{16,0},... | collective-permute-start | bytes 1978376 | tf_op jit(solution)/shard_map/ppermute | solution.py:420
  300.1 72.8 %collective-permute-start.25 = (bf16[2576,128]{1,0:T(8,128)(2,1)}, bf16[2576,128]{1,0:T(8,128)(2,1)}, u32[]{:S(2)}, u32[]{:S(2)}) collective-permute-start(bf16[2576,128]{1,0:T(8,128)(2,1)} %get-tuple-element.137), channel_id=1, source_target_pairs={{0,18},{2,16},{4,22},{6,20},{8,26},{10,24},{12,30},{14,28},{16,2},... | collective-permute-start | bytes 1978376 | tf_op jit(solution)/shard_map/ppermute | solution.py:420
  340.7 114.9 %collective-permute-start.26 = (bf16[2576,128]{1,0:T(8,128)(2,1)}, bf16[2576,128]{1,0:T(8,128)(2,1)}, u32[]{:S(2)}, u32[]{:S(2)}) collective-permute-start(bf16[2576,128]{1,0:T(8,128)(2,1)} %get-tuple-element.138), channel_id=1, source_target_pairs={{0,20},{2,22},{4,16},{6,18},{8,28},{10,30},{12,24},{14,26},{16,4},... | collective-permute-start | bytes 1978376 | tf_op jit(solution)/shard_map/ppermute | solution.py:420
  354.9 130.0 %collective-permute-start.27 = (bf16[2576,128]{1,0:T(8,128)(2,1)}, bf16[2576,128]{1,0:T(8,128)(2,1)}, u32[]{:S(2)}, u32[]{:S(2)}) collective-permute-start(bf16[2576,128]{1,0:T(8,128)(2,1)} %get-tuple-element.139), channel_id=1, source_target_pairs={{0,22},{2,20},{4,18},{6,16},{8,30},{10,28},{12,26},{14,24},{16,6},... | collective-permute-start | bytes 1978376 | tf_op jit(solution)/shard_map/ppermute | solution.py:420
  369.0 130.3 %collective-permute-start.28 = (bf16[2576,128]{1,0:T(8,128)(2,1)}, bf16[2576,128]{1,0:T(8,128)(2,1)}, u32[]{:S(2)}, u32[]{:S(2)}) collective-permute-start(bf16[2576,128]{1,0:T(8,128)(2,1)} %get-tuple-element.140), channel_id=1, source_target_pairs={{0,24},{2,26},{4,28},{6,30},{8,16},{10,18},{12,20},{14,22},{16,8},... | collective-permute-start | bytes 1978376 | tf_op jit(solution)/shard_map/ppermute | solution.py:420
  369.7 143.8 %collective-permute-start.29 = (bf16[2576,128]{1,0:T(8,128)(2,1)}, bf16[2576,128]{1,0:T(8,128)(2,1)}, u32[]{:S(2)}, u32[]{:S(2)}) collective-permute-start(bf16[2576,128]{1,0:T(8,128)(2,1)} %get-tuple-element.141), channel_id=1, source_target_pairs={{0,26},{2,24},{4,30},{6,28},{8,18},{10,16},{12,22},{14,20},{16,10}... | collective-permute-start | bytes 1978376 | tf_op jit(solution)/shard_map/ppermute | solution.py:420
  372.9 155.2 %collective-permute-start.30 = (bf16[2576,128]{1,0:T(8,128)(2,1)}, bf16[2576,128]{1,0:T(8,128)(2,1)}, u32[]{:S(2)}, u32[]{:S(2)}) collective-permute-start(bf16[2576,128]{1,0:T(8,128)(2,1)} %get-tuple-element.142), channel_id=1, source_target_pairs={{0,28},{2,30},{4,24},{6,26},{8,20},{10,22},{12,16},{14,18},{16,12}... | collective-permute-start | bytes 1978376 | tf_op jit(solution)/shard_map/ppermute | solution.py:420
  455.5 86.7 %collective-permute-start.31 = (bf16[2576,128]{1,0:T(8,128)(2,1)}, bf16[2576,128]{1,0:T(8,128)(2,1)}, u32[]{:S(2)}, u32[]{:S(2)}) collective-permute-start(bf16[2576,128]{1,0:T(8,128)(2,1)} %get-tuple-element.143), channel_id=1, source_target_pairs={{0,30},{2,28},{4,26},{6,24},{8,22},{10,20},{12,18},{14,16},{16,14}... | collective-permute-start | bytes 1978376 | tf_op jit(solution)/shard_map/ppermute | solution.py:420
  605.4 47.7 %collective-permute-start.67 = (bf16[2160,128]{1,0:T(8,128)(2,1)S(1)}, bf16[2160,128]{1,0:T(8,128)(2,1)S(1)}, u32[]{:S(2)}, u32[]{:S(2)}) collective-permute-start(bf16[2160,128]{1,0:T(8,128)(2,1)S(1)} %copy-done.58), channel_id=1, source_target_pairs={{0,12},{2,14},{4,8},{6,10},{8,4},{10,6},{12,0},{14,2},{16,28},{18,... | collective-permute-start | bytes 1658888 | tf_op jit(solution)/shard_map/ppermute | solution.py:420
  608.2 56.8 %collective-permute-start.68 = (bf16[2160,128]{1,0:T(8,128)(2,1)S(1)}, bf16[2160,128]{1,0:T(8,128)(2,1)}, u32[]{:S(2)}, u32[]{:S(2)}) collective-permute-start(bf16[2160,128]{1,0:T(8,128)(2,1)S(1)} %copy-done.57), channel_id=1, source_target_pairs={{0,14},{2,12},{4,10},{6,8},{8,6},{10,4},{12,2},{14,0},{16,30},{18,... | collective-permute-start | bytes 1658888 | tf_op jit(solution)/shard_map/ppermute | solution.py:420
  620.1 45.7 %collective-permute-start.69 = (bf16[2160,128]{1,0:T(8,128)(2,1)S(1)}, bf16[2160,128]{1,0:T(8,128)(2,1)}, u32[]{:S(2)}, u32[]{:S(2)}) collective-permute-start(bf16[2160,128]{1,0:T(8,128)(2,1)S(1)} %copy-done.56), channel_id=1, source_target_pairs={{0,16},{2,18},{4,20},{6,22},{8,24},{10,26},{12,28},{14,30},{16,0},... | collective-permute-start | bytes 1658888 | tf_op jit(solution)/shard_map/ppermute | solution.py:420
  620.1 50.4 %collective-permute-start.70 = (bf16[2160,128]{1,0:T(8,128)(2,1)S(1)}, bf16[2160,128]{1,0:T(8,128)(2,1)}, u32[]{:S(2)}, u32[]{:S(2)}) collective-permute-start(bf16[2160,128]{1,0:T(8,128)(2,1)S(1)} %copy-done.55), channel_id=1, source_target_pairs={{0,18},{2,16},{4,22},{6,20},{8,26},{10,24},{12,30},{14,28},{16,2},... | collective-permute-start | bytes 1658888 | tf_op jit(solution)/shard_map/ppermute | solution.py:420
  623.1 115.5 %collective-permute-start.71 = (bf16[2160,128]{1,0:T(8,128)(2,1)S(1)}, bf16[2160,128]{1,0:T(8,128)(2,1)}, u32[]{:S(2)}, u32[]{:S(2)}) collective-permute-start(bf16[2160,128]{1,0:T(8,128)(2,1)S(1)} %copy-done.54), channel_id=1, source_target_pairs={{0,20},{2,22},{4,16},{6,18},{8,28},{10,30},{12,24},{14,26},{16,4},... | collective-permute-start | bytes 1658888 | tf_op jit(solution)/shard_map/ppermute | solution.py:420
  653.1 114.1 %collective-permute-start.72 = (bf16[2160,128]{1,0:T(8,128)(2,1)}, bf16[2160,128]{1,0:T(8,128)(2,1)}, u32[]{:S(2)}, u32[]{:S(2)}) collective-permute-start(bf16[2160,128]{1,0:T(8,128)(2,1)} %get-tuple-element.188), channel_id=1, source_target_pairs={{0,22},{2,20},{4,18},{6,16},{8,30},{10,28},{12,26},{14,24},{16,6},... | collective-permute-start | bytes 1658888 | tf_op jit(solution)/shard_map/ppermute | solution.py:420
  665.0 110.7 %collective-permute-start.73 = (bf16[2160,128]{1,0:T(8,128)(2,1)}, bf16[2160,128]{1,0:T(8,128)(2,1)}, u32[]{:S(2)}, u32[]{:S(2)}) collective-permute-start(bf16[2160,128]{1,0:T(8,128)(2,1)} %get-tuple-element.189), channel_id=1, source_target_pairs={{0,24},{2,26},{4,28},{6,30},{8,16},{10,18},{12,20},{14,22},{16,8},... | collective-permute-start | bytes 1658888 | tf_op jit(solution)/shard_map/ppermute | solution.py:420
  665.7 122.6 %collective-permute-start.74 = (bf16[2160,128]{1,0:T(8,128)(2,1)}, bf16[2160,128]{1,0:T(8,128)(2,1)}, u32[]{:S(2)}, u32[]{:S(2)}) collective-permute-start(bf16[2160,128]{1,0:T(8,128)(2,1)} %get-tuple-element.190), channel_id=1, source_target_pairs={{0,26},{2,24},{4,30},{6,28},{8,18},{10,16},{12,22},{14,20},{16,10}... | collective-permute-start | bytes 1658888 | tf_op jit(solution)/shard_map/ppermute | solution.py:420
  670.5 129.4 %collective-permute-start.75 = (bf16[2160,128]{1,0:T(8,128)(2,1)}, bf16[2160,128]{1,0:T(8,128)(2,1)}, u32[]{:S(2)}, u32[]{:S(2)}) collective-permute-start(bf16[2160,128]{1,0:T(8,128)(2,1)} %get-tuple-element.191), channel_id=1, source_target_pairs={{0,28},{2,30},{4,24},{6,26},{8,20},{10,22},{12,16},{14,18},{16,12}... | collective-permute-start | bytes 1658888 | tf_op jit(solution)/shard_map/ppermute | solution.py:420
  738.5 73.4 %collective-permute-start.76 = (bf16[2160,128]{1,0:T(8,128)(2,1)}, bf16[2160,128]{1,0:T(8,128)(2,1)}, u32[]{:S(2)}, u32[]{:S(2)}) collective-permute-start(bf16[2160,128]{1,0:T(8,128)(2,1)} %get-tuple-element.192), channel_id=1, source_target_pairs={{0,30},{2,28},{4,26},{6,24},{8,22},{10,20},{12,18},{14,16},{16,14}... | collective-permute-start | bytes 1658888 | tf_op jit(solution)/shard_map/ppermute | solution.py:420
  (108 other events, 4289.2 us)
